TPU v7x, 256 devices: a whole 4x4x8 slice. The times are simulated.
256 devices in a mesh: blk: 64 (over x, z, core), grp: 4 (over y).
Axes of the slice: x: 4, y: 4, z: 8, core: 2. Of those that a mesh axis runs over, the one named last changes fastest.
Arguments:
- source_coords: float32 [3, 163840], P(None, ('blk', 'grp')), may hold values from 0 to 64, as said below
- source_values: float32 [3, 163840], P(None, ('blk', 'grp')), may hold values from -48 to 48
- target_coords: float32 [3, 131072], P(None, ('blk', 'grp')), may hold values from 0 to 64, as said below
- target_owner: int32 [131072], P(('blk', 'grp')), may hold values from 0 to 63, as said below
Outputs:
- weights: float32 [3, 163840], P(None, ('blk', 'grp'))
- poly: float32 [3, 4], replicated
- mapped: float32 [3, 131072], P(None, ('blk', 'grp'))
Inputs may be any that keep to these rules, and one draw needn't show every extreme that they name: `source_coords`: source vertex j has its first coordinate between j // 2560 and j // 2560 + 1, and the other two between 0 and 1. `target_coords`: target vertex t has its first coordinate between target_owner[t] and target_owner[t] + 1, and the other two between 0 and 1. target_owner[t] differs from t // 2048 by at most one.
All inputs are finite; a program needn't handle non-finite values.
Results may differ from a plain program's by a relative error of at most 0.0003.
Values sent between devices are 32-bit elements; how exact they have to be, the bound alone decides.
A program may use at most 64 MiB of HBM per device.

v0:
```python
import functools
import math

import jax
import jax.numpy as jnp
from jax import lax
from jax.sharding import Mesh
from jax.sharding import PartitionSpec as P

ITERS = 3
REACH = 2
BLK = ("blk_0", "blk_1", "blk_2")
BLK_GRP = ("blk_0", "blk_1", "blk_2", "grp")


precise = lax.Precision.HIGHEST
thin_factor = 0.6
tiny = 1e-06


def copy_for_each(x, axis):
    copies = jnp.broadcast_to(x, (lax.axis_size(axis), *x.shape))
    return lax.all_to_all(copies, axis, split_axis=0, concat_axis=0, tiled=True)


def joined_along(parts, dim):
    parts = jnp.moveaxis(parts, 0, dim)
    dims = parts.shape
    return parts.reshape(*dims[:dim], dims[dim] * dims[dim + 1], *dims[dim + 2 :])


def collect(x, axis, dim):
    parts = copy_for_each(x, axis)
    return joined_along(parts, dim)


def from_behind(value, axis, steps):
    count = lax.axis_size(axis)
    initial, last = (max(0, -steps), min(count, count - steps))
    return lax.ppermute(value, axis, [(source, source + steps) for source in range(initial, last)])


def over_axes(x, axes):
    return functools.reduce(lax.psum, axes, x)


def kernel_tile(rows, cols, stretch):
    along = rows[0][None, :] - cols[0][:, None]
    across = rows[1][None, :] - cols[1][:, None]
    upward = rows[2][None, :] - cols[2][:, None]
    return jnp.exp(-(thin_factor * along * along + stretch * (across * across + upward * upward)))


def basis(points, partitions, sources):
    ones = jnp.ones_like(points[0])
    stacked = jnp.stack(
        [ones, 2.0 * points[0] / partitions - 1.0, 2.0 * points[1] - 1.0, 2.0 * points[2] - 1.0]
    )
    return stacked / math.sqrt(sources)


def least_squares(hessenberg, beta):
    count = len(hessenberg)
    right_side = [beta] + [jnp.zeros_like(beta) for k in range(count)]
    upper = []
    cosines = []
    sines = []
    for k in range(count):
        column = list(hessenberg[k])
        for i in range(k):
            top = cosines[i] * column[i] + sines[i] * column[i + 1]
            lower = -sines[i] * column[i] + cosines[i] * column[i + 1]
            column[i] = top
            column[i + 1] = lower
        radius = jnp.sqrt(column[k] * column[k] + column[k + 1] * column[k + 1])
        cosine = column[k] / radius
        sine = column[k + 1] / radius
        column[k] = radius
        cosines.append(cosine)
        sines.append(sine)
        right_side[k + 1] = -sine * right_side[k]
        right_side[k] = cosine * right_side[k]
        upper.append(column[: k + 1])
    solved = [None] * count
    for k in reversed(range(count)):
        running = right_side[k]
        for j in range(k + 1, count):
            running = running - upper[j][k] * solved[j]
        solved[k] = running / upper[k][k]
    return solved


def near_slabs(block, reach):
    slab = collect(block, "grp", 1)
    pieces = []
    for offset in range(-reach, reach + 1):
        if offset == 0:
            pieces.append(slab)
        else:
            pieces.append(from_behind(slab, BLK, -offset))
    return jnp.stack(pieces)


def apply_near(rows, near_coords, near_values, owners, first_slab, stretch, reach):
    labels = jnp.arange(near_coords.shape[0], dtype=jnp.int32) + first_slab

    def add_slab(running, item):
        cols, values, slab = item
        tile = kernel_tile(rows, cols, stretch)
        if owners is not None:
            tile = jnp.where((jnp.abs(owners - slab) <= reach)[None, :], tile, 0.0)
        return (
            running + jnp.dot(values, tile, precision=precise, preferred_element_type=jnp.float32),
            None,
        )

    start = jnp.zeros((near_values.shape[1], rows.shape[1]), jnp.float32)
    result, unused = lax.scan(add_slab, start, (near_coords, near_values, labels))
    return result


def shards(source_coords, source_values, target_coords, target_owner):
    reach = REACH
    own_rows = source_coords.shape[1]
    slab_len = own_rows * lax.axis_size("grp")
    partitions = lax.axis_size(BLK)
    sources = slab_len * partitions
    stretch = 4.0 * slab_len
    here = lax.axis_index(BLK)
    poly_src = basis(source_coords, partitions, sources)
    start_sq, start_moment = (
        over_axes(jnp.sum(source_values * source_values, axis=1), BLK_GRP),
        over_axes(
            jnp.dot(
                source_values, poly_src.T, precision=precise, preferred_element_type=jnp.float32
            ),
            BLK_GRP,
        ),
    )
    beta = jnp.sqrt(start_sq + tiny)
    heads = [source_values / beta[:, None]]
    tails = [jnp.zeros_like(start_moment)]
    moments = [start_moment / beta[:, None]]
    hessenberg = []
    for k in range(ITERS):
        both_near = near_slabs(jnp.concatenate([source_coords, heads[k]], axis=0), reach)
        cols = both_near[:, :3]
        values_near = both_near[:, 3:]
        image_head = apply_near(
            source_coords, cols, values_near, None, here - reach, stretch, reach
        ) + jnp.dot(tails[k], poly_src, precision=precise, preferred_element_type=jnp.float32)
        image_tail = moments[k]
        column = []
        local_dots = jnp.stack(
            [jnp.sum(heads[i] * image_head, axis=1) for i in range(k + 1)], axis=1
        )
        head_dots, image_sq, image_moment = (
            over_axes(local_dots, BLK_GRP),
            over_axes(jnp.sum(image_head * image_head, axis=1), BLK_GRP),
            over_axes(
                jnp.dot(
                    image_head, poly_src.T, precision=precise, preferred_element_type=jnp.float32
                ),
                BLK_GRP,
            ),
        )
        full_sq = image_sq + jnp.sum(image_tail * image_tail, axis=1)
        rest_head = image_head
        rest_tail = image_tail
        rest_moment = image_moment
        for i in range(k + 1):
            factor = head_dots[:, i] + jnp.sum(tails[i] * image_tail, axis=1)
            full_sq = full_sq - factor * factor
            rest_head = rest_head - factor[:, None] * heads[i]
            rest_tail = rest_tail - factor[:, None] * tails[i]
            rest_moment = rest_moment - factor[:, None] * moments[i]
            column.append(factor)
        length = jnp.sqrt(full_sq + tiny)
        column.append(length)
        hessenberg.append(column)
        heads.append(rest_head / length[:, None])
        tails.append(rest_tail / length[:, None])
        moments.append(rest_moment / length[:, None])
    solved = least_squares(hessenberg, beta)
    weights = solved[0][:, None] * heads[0]
    poly = solved[0][:, None] * tails[0]
    for k in range(1, ITERS):
        weights = weights + solved[k][:, None] * heads[k]
        poly = poly + solved[k][:, None] * tails[k]
    joined_near = near_slabs(jnp.concatenate([source_coords, weights], axis=0), reach + 1)
    cols_far = joined_near[:, :3]
    weights_near = joined_near[:, 3:]
    poly_tgt = basis(target_coords, partitions, sources)
    mapped = apply_near(
        target_coords, cols_far, weights_near, target_owner, here - reach - 1, stretch, reach
    )
    mapped = mapped + jnp.dot(poly, poly_tgt, precision=precise, preferred_element_type=jnp.float32)
    return (weights, poly, mapped)


def solution(mesh):
    finer = Mesh(
        mesh.devices.reshape(4, 8, 2, mesh.shape["grp"]), ("blk_0", "blk_1", "blk_2", "grp")
    )
    in_specs = (P(None, BLK_GRP), P(None, BLK_GRP), P(None, BLK_GRP), P(BLK_GRP))
    out_specs = (P(None, BLK_GRP), P(), P(None, BLK_GRP))
    return jax.shard_map(
        shards, mesh=finer, in_specs=in_specs, out_specs=out_specs, check_vma=False
    )
```

profile of v0, /device:TPU:1, one launch (start us, length us, event | category | flops | bytes accessed | tf_op | source)
XLA Modules:
  0.0 403.0 jit_solution(4838088872800558235)
XLA Ops:
  1.5 9.3 %psum.280 = f32[3]{0:T(128)S(1)} all-reduce(f32[3]{0:T(128)S(1)} %multiply_reduce_fusion.9), channel_id=1, replica_groups=mesh['blk_0'=4,'blk_1'=8,'blk_2'=2,'grp'=4] {'blk_0'}, use_global_device_ids=true, to_apply=%region_1.0 | all-reduce | flops 3 | bytes 24 | tf_op jit(solution)/shard_map/psum | solution.py:44
  10.7 16.2 %psum.281 = f32[3]{0:T(128)S(1)} all-reduce(f32[3]{0:T(128)S(1)} %psum.280), channel_id=1, replica_groups=mesh['blk_0'=4,'blk_1'=8,'blk_2'=2,'grp'=4] {'blk_1'}, use_global_device_ids=true, to_apply=%region_2.0 | all-reduce | flops 3 | bytes 24 | tf_op jit(solution)/shard_map/psum | solution.py:44
  27.0 8.6 %psum.282 = f32[3]{0:T(128)S(1)} all-reduce(f32[3]{0:T(128)S(1)} %psum.281), channel_id=1, replica_groups=mesh['blk_0'=4,'blk_1'=8,'blk_2'=2,'grp'=4] {'blk_2'}, use_global_device_ids=true, to_apply=%region_3.0 | all-reduce | flops 3 | bytes 24 | tf_op jit(solution)/shard_map/psum | solution.py:44
  35.5 8.7 %psum.283 = f32[3]{0:T(128)S(1)} all-reduce(f32[3]{0:T(128)S(1)} %psum.282), channel_id=1, replica_groups=mesh['blk_0'=4,'blk_1'=8,'blk_2'=2,'grp'=4] {'grp'}, use_global_device_ids=true, to_apply=%region_4.0 | all-reduce | flops 3 | bytes 24 | tf_op jit(solution)/shard_map/psum | solution.py:44
  56.5 6.3 %collective-permute-start.1 = (f32[6,2560]{1,0:T(8,128)S(1)}, f32[6,2560]{1,0:T(8,128)S(1)}, u32[]{:S(2)}, u32[]{:S(2)}) collective-permute-start(f32[6,2560]{1,0:T(8,128)S(1)} %bitcast.227), channel_id=1, source_target_pairs={{0,4},{4,8},{8,12},{12,16},{16,20},{20,24},{24,28},{28,32},{32,36}... | collective-permute-start | bytes 184328 | tf_op jit(solution)/shard_map/ppermute | solution.py:40
  70.7 29.7 %while.44 = (s32[]{:T(128)}, f32[3,640]{1,0:T(4,128)S(1)}, f32[5,3,2560]{2,1,0:T(4,128)S(1)}, f32[3,640]{1,0:T(4,128)S(1)}, f32[5,3,2560]{2,1,0:T(4,128)S(1)}, /*index=5*/s32[]{:T(128)}, s32[]{:T(128)}, s32[]{}, s32[]{}) while((s32[]{:T(128)}, f32[3,640]{1,0:T(4,128)S(1)}, f32[5,3,2560]{2,1,0:T(4,128)S(1)}, ...), condition=%wide.region_6.0_spmd.clone, body=%wide.region_5.0_spmd.clone.sunk | while | flops 77008640 | bytes 184975 | solution.py:118
  70.9 5.8 %fusion.163 = f32[3,640]{1,0:T(4,128)S(1)} fusion(f32[2560]{0:T(1024)S(1)} %get-tuple-element.496, f32[640]{0:T(1024)S(1)} %get-tuple-element.497, f32[2560]{0:T(1024)S(1)} %get-tuple-element.498, f32[640]{0:T(1024)S(1)} %get-tuple-element.499, f32[2560]{0:T(1024)S(1)} %get-tuple-element.500, f32[640]{0:T(1024)S(1)} %get-tuple-element.501, ...), kind=kOutput, calls=%fused_computation.20.clone.1 | convolution fusion | flops 77008640 | bytes 108037 | tf_op jit(solution)/shard_map/while/body/eval_jaxpr/dot_general | solution.py:113
  76.8 5.8 %fusion.163 = f32[3,640]{1,0:T(4,128)S(1)} fusion(f32[2560]{0:T(1024)S(1)} %get-tuple-element.496, f32[640]{0:T(1024)S(1)} %get-tuple-element.497, f32[2560]{0:T(1024)S(1)} %get-tuple-element.498, f32[640]{0:T(1024)S(1)} %get-tuple-element.499, f32[2560]{0:T(1024)S(1)} %get-tuple-element.500, f32[640]{0:T(1024)S(1)} %get-tuple-element.501, ...), kind=kOutput, calls=%fused_computation.20.clone.1 | convolution fusion | flops 77008640 | bytes 108037 | tf_op jit(solution)/shard_map/while/body/eval_jaxpr/dot_general | solution.py:113
  82.7 5.8 %fusion.163 = f32[3,640]{1,0:T(4,128)S(1)} fusion(f32[2560]{0:T(1024)S(1)} %get-tuple-element.496, f32[640]{0:T(1024)S(1)} %get-tuple-element.497, f32[2560]{0:T(1024)S(1)} %get-tuple-element.498, f32[640]{0:T(1024)S(1)} %get-tuple-element.499, f32[2560]{0:T(1024)S(1)} %get-tuple-element.500, f32[640]{0:T(1024)S(1)} %get-tuple-element.501, ...), kind=kOutput, calls=%fused_computation.20.clone.1 | convolution fusion | flops 77008640 | bytes 108037 | tf_op jit(solution)/shard_map/while/body/eval_jaxpr/dot_general | solution.py:113
  88.7 5.8 %fusion.163 = f32[3,640]{1,0:T(4,128)S(1)} fusion(f32[2560]{0:T(1024)S(1)} %get-tuple-element.496, f32[640]{0:T(1024)S(1)} %get-tuple-element.497, f32[2560]{0:T(1024)S(1)} %get-tuple-element.498, f32[640]{0:T(1024)S(1)} %get-tuple-element.499, f32[2560]{0:T(1024)S(1)} %get-tuple-element.500, f32[640]{0:T(1024)S(1)} %get-tuple-element.501, ...), kind=kOutput, calls=%fused_computation.20.clone.1 | convolution fusion | flops 77008640 | bytes 108037 | tf_op jit(solution)/shard_map/while/body/eval_jaxpr/dot_general | solution.py:113
  94.6 5.8 %fusion.163 = f32[3,640]{1,0:T(4,128)S(1)} fusion(f32[2560]{0:T(1024)S(1)} %get-tuple-element.496, f32[640]{0:T(1024)S(1)} %get-tuple-element.497, f32[2560]{0:T(1024)S(1)} %get-tuple-element.498, f32[640]{0:T(1024)S(1)} %get-tuple-element.499, f32[2560]{0:T(1024)S(1)} %get-tuple-element.500, f32[640]{0:T(1024)S(1)} %get-tuple-element.501, ...), kind=kOutput, calls=%fused_computation.20.clone.1 | convolution fusion | flops 77008640 | bytes 108037 | tf_op jit(solution)/shard_map/while/body/eval_jaxpr/dot_general | solution.py:113
  100.7 6.5 %all-reduce.8 = (f32[3]{0:T(128)S(1)}, f32[3,4]{1,0:T(4,128)S(1)}, f32[3,1]{0,1:T(1,128)S(1)}) all-reduce(f32[3]{0:T(128)S(1)} %get-tuple-element.232, f32[3,4]{1,0:T(4,128)S(1)} %convolution_bitcast_fusion, f32[3,1]{0,1:T(1,128)S(1)} %bitcast.242), channel_id=1, replica_groups=mesh['blk_0'=4,'blk_1'=8,'blk_2'=2,'grp'=4] {'blk_0'}, use_global_device_ids=true, to_apply=%region_18.19 | all-reduce | flops 18 | bytes 144 | tf_op jit(solution)/shard_map/psum | solution.py:44
  107.2 14.2 %all-reduce.2 = (f32[3]{0:T(128)S(1)}, f32[3,4]{1,0:T(4,128)S(1)}, f32[3,1]{0,1:T(1,128)S(1)}) all-reduce(f32[3]{0:T(128)S(1)} %get-tuple-element.310, f32[3,4]{1,0:T(4,128)S(1)} %get-tuple-element.311, f32[3,1]{0,1:T(1,128)S(1)} %get-tuple-element.312), channel_id=1, replica_groups=mesh['blk_0'=4,'blk_1'=8,'blk_2'=2,'grp'=4] {'blk_1'}, use_global_device_ids=true, to_apply=%region_19.20 | all-reduce | flops 18 | bytes 144 | tf_op jit(solution)/shard_map/psum | solution.py:44
  121.4 10.8 %all-reduce.11 = (f32[3]{0:T(128)S(1)}, f32[3,4]{1,0:T(4,128)S(1)}, f32[3,1]{0,1:T(1,128)S(1)}) all-reduce(f32[3]{0:T(128)S(1)} %get-tuple-element.292, f32[3,4]{1,0:T(4,128)S(1)} %get-tuple-element.293, f32[3,1]{0,1:T(1,128)S(1)} %get-tuple-element.294), channel_id=1, replica_groups=mesh['blk_0'=4,'blk_1'=8,'blk_2'=2,'grp'=4] {'blk_2'}, use_global_device_ids=true, to_apply=%region_20.21 | all-reduce | flops 18 | bytes 144 | tf_op jit(solution)/shard_map/psum | solution.py:44
  132.2 6.8 %all-reduce.5 = (f32[3]{0:T(128)S(1)}, f32[3,4]{1,0:T(4,128)S(1)}, f32[3,1]{0,1:T(1,128)S(1)}) all-reduce(f32[3]{0:T(128)S(1)} %get-tuple-element.319, f32[3,4]{1,0:T(4,128)S(1)} %get-tuple-element.320, f32[3,1]{0,1:T(1,128)S(1)} %get-tuple-element.321), channel_id=1, replica_groups=mesh['blk_0'=4,'blk_1'=8,'blk_2'=2,'grp'=4] {'grp'}, use_global_device_ids=true, to_apply=%region_21.22 | all-reduce | flops 18 | bytes 144 | tf_op jit(solution)/shard_map/psum | solution.py:44
  143.3 4.5 %all-to-all-done.1 = f32[4,6,640]{2,1,0:T(8,128)S(1)} async-done(((f32[4,6,640]{2,1,0:T(8,128)}), f32[4,6,640]{2,1,0:T(8,128)S(1)}, u32[]{:S(2)}, u32[]{:S(2)}) %all-to-all-start.1) | async-done | bytes 61472 | tf_op jit(solution)/shard_map/all_to_all | solution.py:23
  149.3 6.5 %collective-permute-start.5 = (f32[6,2560]{1,0:T(8,128)S(1)}, f32[6,2560]{1,0:T(8,128)S(1)}, u32[]{:S(2)}, u32[]{:S(2)}) collective-permute-start(f32[6,2560]{1,0:T(8,128)S(1)} %bitcast.215), channel_id=1, source_target_pairs={{0,4},{4,8},{8,12},{12,16},{16,20},{20,24},{24,28},{28,32},{32,36}... | collective-permute-start | bytes 184328 | tf_op jit(solution)/shard_map/ppermute | solution.py:40
  163.6 29.7 %while.45 = (s32[]{:T(128)}, f32[3,640]{1,0:T(4,128)S(1)}, f32[5,3,2560]{2,1,0:T(4,128)S(1)}, f32[3,640]{1,0:T(4,128)S(1)}, f32[5,3,2560]{2,1,0:T(4,128)S(1)}, /*index=5*/s32[]{:T(128)}, s32[]{:T(128)}, s32[]{}, s32[]{}) while((s32[]{:T(128)}, f32[3,640]{1,0:T(4,128)S(1)}, f32[5,3,2560]{2,1,0:T(4,128)S(1)}, ...), condition=%wide.region_24.25_spmd.clone, body=%wide.region_23.24_spmd.clone.sunk | while | flops 77008640 | bytes 184975 | solution.py:118
  163.7 5.8 %fusion.166 = f32[3,640]{1,0:T(4,128)S(1)} fusion(f32[2560]{0:T(1024)S(1)} %get-tuple-element.507, f32[640]{0:T(1024)S(1)} %get-tuple-element.508, f32[2560]{0:T(1024)S(1)} %get-tuple-element.509, f32[640]{0:T(1024)S(1)} %get-tuple-element.510, f32[2560]{0:T(1024)S(1)} %get-tuple-element.511, f32[640]{0:T(1024)S(1)} %get-tuple-element.512, ...), kind=kOutput, calls=%fused_computation.52.clone.1 | convolution fusion | flops 77008640 | bytes 108037 | tf_op jit(solution)/shard_map/while/body/eval_jaxpr/dot_general | solution.py:113
  169.7 5.8 %fusion.166 = f32[3,640]{1,0:T(4,128)S(1)} fusion(f32[2560]{0:T(1024)S(1)} %get-tuple-element.507, f32[640]{0:T(1024)S(1)} %get-tuple-element.508, f32[2560]{0:T(1024)S(1)} %get-tuple-element.509, f32[640]{0:T(1024)S(1)} %get-tuple-element.510, f32[2560]{0:T(1024)S(1)} %get-tuple-element.511, f32[640]{0:T(1024)S(1)} %get-tuple-element.512, ...), kind=kOutput, calls=%fused_computation.52.clone.1 | convolution fusion | flops 77008640 | bytes 108037 | tf_op jit(solution)/shard_map/while/body/eval_jaxpr/dot_general | solution.py:113
  175.6 5.8 %fusion.166 = f32[3,640]{1,0:T(4,128)S(1)} fusion(f32[2560]{0:T(1024)S(1)} %get-tuple-element.507, f32[640]{0:T(1024)S(1)} %get-tuple-element.508, f32[2560]{0:T(1024)S(1)} %get-tuple-element.509, f32[640]{0:T(1024)S(1)} %get-tuple-element.510, f32[2560]{0:T(1024)S(1)} %get-tuple-element.511, f32[640]{0:T(1024)S(1)} %get-tuple-element.512, ...), kind=kOutput, calls=%fused_computation.52.clone.1 | convolution fusion | flops 77008640 | bytes 108037 | tf_op jit(solution)/shard_map/while/body/eval_jaxpr/dot_general | solution.py:113
  181.6 5.8 %fusion.166 = f32[3,640]{1,0:T(4,128)S(1)} fusion(f32[2560]{0:T(1024)S(1)} %get-tuple-element.507, f32[640]{0:T(1024)S(1)} %get-tuple-element.508, f32[2560]{0:T(1024)S(1)} %get-tuple-element.509, f32[640]{0:T(1024)S(1)} %get-tuple-element.510, f32[2560]{0:T(1024)S(1)} %get-tuple-element.511, f32[640]{0:T(1024)S(1)} %get-tuple-element.512, ...), kind=kOutput, calls=%fused_computation.52.clone.1 | convolution fusion | flops 77008640 | bytes 108037 | tf_op jit(solution)/shard_map/while/body/eval_jaxpr/dot_general | solution.py:113
  187.5 5.8 %fusion.166 = f32[3,640]{1,0:T(4,128)S(1)} fusion(f32[2560]{0:T(1024)S(1)} %get-tuple-element.507, f32[640]{0:T(1024)S(1)} %get-tuple-element.508, f32[2560]{0:T(1024)S(1)} %get-tuple-element.509, f32[640]{0:T(1024)S(1)} %get-tuple-element.510, f32[2560]{0:T(1024)S(1)} %get-tuple-element.511, f32[640]{0:T(1024)S(1)} %get-tuple-element.512, ...), kind=kOutput, calls=%fused_computation.52.clone.1 | convolution fusion | flops 77008640 | bytes 108037 | tf_op jit(solution)/shard_map/while/body/eval_jaxpr/dot_general | solution.py:113
  193.7 7.6 %all-reduce.7 = (f32[3]{0:T(128)S(1)}, f32[3,4]{1,0:T(4,128)S(1)}, f32[3,2]{0,1:T(2,128)S(1)}) all-reduce(f32[3]{0:T(128)S(1)} %get-tuple-element.229, f32[3,4]{1,0:T(4,128)S(1)} %fusion.135, f32[3,2]{0,1:T(2,128)S(1)} %pad_maximum_fusion.5), channel_id=1, replica_groups=mesh['blk_0'=4,'blk_1'=8,'blk_2'=2,'grp'=4] {'blk_0'}, use_global_device_ids=true, to_apply=%region_38.39 | all-reduce | flops 21 | bytes 168 | tf_op jit(solution)/shard_map/psum | solution.py:44
  201.3 13.4 %all-reduce.1 = (f32[3]{0:T(128)S(1)}, f32[3,4]{1,0:T(4,128)S(1)}, f32[3,2]{0,1:T(2,128)S(1)}) all-reduce(f32[3]{0:T(128)S(1)} %get-tuple-element.307, f32[3,4]{1,0:T(4,128)S(1)} %get-tuple-element.308, f32[3,2]{0,1:T(2,128)S(1)} %get-tuple-element.309), channel_id=1, replica_groups=mesh['blk_0'=4,'blk_1'=8,'blk_2'=2,'grp'=4] {'blk_1'}, use_global_device_ids=true, to_apply=%region_39.40 | all-reduce | flops 21 | bytes 168 | tf_op jit(solution)/shard_map/psum | solution.py:44
  214.7 10.5 %all-reduce.10 = (f32[3]{0:T(128)S(1)}, f32[3,4]{1,0:T(4,128)S(1)}, f32[3,2]{0,1:T(2,128)S(1)}) all-reduce(f32[3]{0:T(128)S(1)} %get-tuple-element.289, f32[3,4]{1,0:T(4,128)S(1)} %get-tuple-element.290, f32[3,2]{0,1:T(2,128)S(1)} %get-tuple-element.291), channel_id=1, replica_groups=mesh['blk_0'=4,'blk_1'=8,'blk_2'=2,'grp'=4] {'blk_2'}, use_global_device_ids=true, to_apply=%region_40.41 | all-reduce | flops 21 | bytes 168 | tf_op jit(solution)/shard_map/psum | solution.py:44
  225.2 6.8 %all-reduce.4 = (f32[3]{0:T(128)S(1)}, f32[3,4]{1,0:T(4,128)S(1)}, f32[3,2]{0,1:T(2,128)S(1)}) all-reduce(f32[3]{0:T(128)S(1)} %get-tuple-element.316, f32[3,4]{1,0:T(4,128)S(1)} %get-tuple-element.317, f32[3,2]{0,1:T(2,128)S(1)} %get-tuple-element.318), channel_id=1, replica_groups=mesh['blk_0'=4,'blk_1'=8,'blk_2'=2,'grp'=4] {'grp'}, use_global_device_ids=true, to_apply=%region_41.42 | all-reduce | flops 21 | bytes 168 | tf_op jit(solution)/shard_map/psum | solution.py:44
  242.2 6.4 %collective-permute-start.9 = (f32[6,2560]{1,0:T(8,128)S(1)}, f32[6,2560]{1,0:T(8,128)S(1)}, u32[]{:S(2)}, u32[]{:S(2)}) collective-permute-start(f32[6,2560]{1,0:T(8,128)S(1)} %bitcast.232), channel_id=1, source_target_pairs={{0,4},{4,8},{8,12},{12,16},{16,20},{20,24},{24,28},{28,32},{32,36}... | collective-permute-start | bytes 184328 | tf_op jit(solution)/shard_map/ppermute | solution.py:40
  256.4 29.7 %while.46 = (s32[]{:T(128)}, f32[3,640]{1,0:T(4,128)S(1)}, f32[5,3,2560]{2,1,0:T(4,128)S(1)}, f32[3,640]{1,0:T(4,128)S(1)}, f32[5,3,2560]{2,1,0:T(4,128)S(1)}, /*index=5*/s32[]{:T(128)}, s32[]{:T(128)}, s32[]{}, s32[]{}) while((s32[]{:T(128)}, f32[3,640]{1,0:T(4,128)S(1)}, f32[5,3,2560]{2,1,0:T(4,128)S(1)}, ...), condition=%wide.region_44.45_spmd.clone, body=%wide.region_43.44_spmd.clone.sunk | while | flops 77008640 | bytes 184975 | solution.py:118
  256.6 5.8 %fusion.169 = f32[3,640]{1,0:T(4,128)S(1)} fusion(f32[2560]{0:T(1024)S(1)} %get-tuple-element.518, f32[640]{0:T(1024)S(1)} %get-tuple-element.519, f32[2560]{0:T(1024)S(1)} %get-tuple-element.520, f32[640]{0:T(1024)S(1)} %get-tuple-element.521, f32[2560]{0:T(1024)S(1)} %get-tuple-element.522, f32[640]{0:T(1024)S(1)} %get-tuple-element.523, ...), kind=kOutput, calls=%fused_computation.84.clone.1 | convolution fusion | flops 77008640 | bytes 108037 | tf_op jit(solution)/shard_map/while/body/eval_jaxpr/dot_general | solution.py:113
  262.5 5.8 %fusion.169 = f32[3,640]{1,0:T(4,128)S(1)} fusion(f32[2560]{0:T(1024)S(1)} %get-tuple-element.518, f32[640]{0:T(1024)S(1)} %get-tuple-element.519, f32[2560]{0:T(1024)S(1)} %get-tuple-element.520, f32[640]{0:T(1024)S(1)} %get-tuple-element.521, f32[2560]{0:T(1024)S(1)} %get-tuple-element.522, f32[640]{0:T(1024)S(1)} %get-tuple-element.523, ...), kind=kOutput, calls=%fused_computation.84.clone.1 | convolution fusion | flops 77008640 | bytes 108037 | tf_op jit(solution)/shard_map/while/body/eval_jaxpr/dot_general | solution.py:113
  268.5 5.8 %fusion.169 = f32[3,640]{1,0:T(4,128)S(1)} fusion(f32[2560]{0:T(1024)S(1)} %get-tuple-element.518, f32[640]{0:T(1024)S(1)} %get-tuple-element.519, f32[2560]{0:T(1024)S(1)} %get-tuple-element.520, f32[640]{0:T(1024)S(1)} %get-tuple-element.521, f32[2560]{0:T(1024)S(1)} %get-tuple-element.522, f32[640]{0:T(1024)S(1)} %get-tuple-element.523, ...), kind=kOutput, calls=%fused_computation.84.clone.1 | convolution fusion | flops 77008640 | bytes 108037 | tf_op jit(solution)/shard_map/while/body/eval_jaxpr/dot_general | solution.py:113
  274.4 5.8 %fusion.169 = f32[3,640]{1,0:T(4,128)S(1)} fusion(f32[2560]{0:T(1024)S(1)} %get-tuple-element.518, f32[640]{0:T(1024)S(1)} %get-tuple-element.519, f32[2560]{0:T(1024)S(1)} %get-tuple-element.520, f32[640]{0:T(1024)S(1)} %get-tuple-element.521, f32[2560]{0:T(1024)S(1)} %get-tuple-element.522, f32[640]{0:T(1024)S(1)} %get-tuple-element.523, ...), kind=kOutput, calls=%fused_computation.84.clone.1 | convolution fusion | flops 77008640 | bytes 108037 | tf_op jit(solution)/shard_map/while/body/eval_jaxpr/dot_general | solution.py:113
  280.3 5.8 %fusion.169 = f32[3,640]{1,0:T(4,128)S(1)} fusion(f32[2560]{0:T(1024)S(1)} %get-tuple-element.518, f32[640]{0:T(1024)S(1)} %get-tuple-element.519, f32[2560]{0:T(1024)S(1)} %get-tuple-element.520, f32[640]{0:T(1024)S(1)} %get-tuple-element.521, f32[2560]{0:T(1024)S(1)} %get-tuple-element.522, f32[640]{0:T(1024)S(1)} %get-tuple-element.523, ...), kind=kOutput, calls=%fused_computation.84.clone.1 | convolution fusion | flops 77008640 | bytes 108037 | tf_op jit(solution)/shard_map/while/body/eval_jaxpr/dot_general | solution.py:113
  286.5 8.8 %all-reduce.6 = (f32[3]{0:T(128)S(1)}, f32[3,4]{1,0:T(4,128)S(1)}, f32[3,3]{0,1:T(4,128)S(1)}) all-reduce(f32[3]{0:T(128)S(1)} %get-tuple-element.225, f32[3,4]{1,0:T(4,128)S(1)} %fusion.134, f32[3,3]{0,1:T(4,128)S(1)} %pad_maximum_fusion.4), channel_id=1, replica_groups=mesh['blk_0'=4,'blk_1'=8,'blk_2'=2,'grp'=4] {'blk_0'}, use_global_device_ids=true, to_apply=%region_60.61 | all-reduce | flops 24 | bytes 192 | tf_op jit(solution)/shard_map/psum | solution.py:44
  295.4 13.6 %all-reduce = (f32[3]{0:T(128)S(1)}, f32[3,4]{1,0:T(4,128)S(1)}, f32[3,3]{0,1:T(4,128)S(1)}) all-reduce(f32[3]{0:T(128)S(1)} %get-tuple-element.304, f32[3,4]{1,0:T(4,128)S(1)} %get-tuple-element.305, f32[3,3]{0,1:T(4,128)S(1)} %get-tuple-element.306), channel_id=1, replica_groups=mesh['blk_0'=4,'blk_1'=8,'blk_2'=2,'grp'=4] {'blk_1'}, use_global_device_ids=true, to_apply=%region_61.62 | all-reduce | flops 24 | bytes 192 | tf_op jit(solution)/shard_map/psum | solution.py:44
  309.0 10.5 %all-reduce.9 = (f32[3]{0:T(128)S(1)}, f32[3,4]{1,0:T(4,128)S(1)}, f32[3,3]{0,1:T(4,128)S(1)}) all-reduce(f32[3]{0:T(128)S(1)} %get-tuple-element.286, f32[3,4]{1,0:T(4,128)S(1)} %get-tuple-element.287, f32[3,3]{0,1:T(4,128)S(1)} %get-tuple-element.288), channel_id=1, replica_groups=mesh['blk_0'=4,'blk_1'=8,'blk_2'=2,'grp'=4] {'blk_2'}, use_global_device_ids=true, to_apply=%region_62.63 | all-reduce | flops 24 | bytes 192 | tf_op jit(solution)/shard_map/psum | solution.py:44
  319.6 6.9 %all-reduce.3 = (f32[3]{0:T(128)S(1)}, f32[3,4]{1,0:T(4,128)S(1)}, f32[3,3]{0,1:T(4,128)S(1)}) all-reduce(f32[3]{0:T(128)S(1)} %get-tuple-element.313, f32[3,4]{1,0:T(4,128)S(1)} %get-tuple-element.314, f32[3,3]{0,1:T(4,128)S(1)} %get-tuple-element.315), channel_id=1, replica_groups=mesh['blk_0'=4,'blk_1'=8,'blk_2'=2,'grp'=4] {'grp'}, use_global_device_ids=true, to_apply=%region_63.64 | all-reduce | flops 24 | bytes 192 | tf_op jit(solution)/shard_map/psum | solution.py:44
  330.9 4.5 %all-to-all-done.3 = f32[4,6,640]{2,1,0:T(8,128)S(1)} async-done(((f32[4,6,640]{2,1,0:T(8,128)}), f32[4,6,640]{2,1,0:T(8,128)S(1)}, u32[]{:S(2)}, u32[]{:S(2)}) %all-to-all-start.3) | async-done | bytes 61472 | tf_op jit(solution)/shard_map/all_to_all | solution.py:23
  335.4 5.3 %collective-permute-start.12 = (f32[6,2560]{1,0:T(8,128)S(1)}, f32[6,2560]{1,0:T(8,128)S(1)}, u32[]{:S(2)}, u32[]{:S(2)}) collective-permute-start(f32[6,2560]{1,0:T(8,128)S(1)} %bitcast.219), channel_id=1, source_target_pairs={{0,12},{4,16},{8,20},{12,24},{16,28},{20,32},{24,36},{28,40},{32,4... | collective-permute-start | bytes 184328 | tf_op jit(solution)/shard_map/ppermute | solution.py:40
  358.0 44.2 %while.47 = (s32[]{:T(128)}, f32[3,512]{1,0:T(4,128)S(1)}, f32[7,3,2560]{2,1,0:T(4,128)S(1)}, s32[7]{0:T(128)S(1)}, s32[512]{0:T(512)S(1)}, /*index=5*/f32[3,512...) while((s32[]{:T(128)}, f32[3,512]{1,0:T(4,128)S(1)}, ...), condition=%wide.region_66.67_spmd.clone, body=%wide.region_65.66_spmd.clone.sunk | while | flops 62919172 | bytes 175279 | solution.py:118
  359.5 4.8 %fusion.173 = f32[3,512]{1,0:T(4,128)S(1)} fusion(f32[2560]{0:T(1024)S(1)} %get-tuple-element.531, f32[512]{0:T(512)S(1)} %bitcast.237, f32[2560]{0:T(1024)S(1)} %get-tuple-element.533, f32[512]{0:T(512)S(1)} %bitcast.238, f32[2560]{0:T(1024)S(1)} %get-tuple-element.535, f32[512]{0:T(512)S(1)} %bitcast.236, ...), kind=kOutput, calls=%fused_computation.119.clone.1 | convolution fusion | flops 62917632 | bytes 98821 | tf_op jit(solution)/shard_map/while/body/eval_jaxpr/dot_general | solution.py:113
  365.8 4.8 %fusion.173 = f32[3,512]{1,0:T(4,128)S(1)} fusion(f32[2560]{0:T(1024)S(1)} %get-tuple-element.531, f32[512]{0:T(512)S(1)} %bitcast.237, f32[2560]{0:T(1024)S(1)} %get-tuple-element.533, f32[512]{0:T(512)S(1)} %bitcast.238, f32[2560]{0:T(1024)S(1)} %get-tuple-element.535, f32[512]{0:T(512)S(1)} %bitcast.236, ...), kind=kOutput, calls=%fused_computation.119.clone.1 | convolution fusion | flops 62917632 | bytes 98821 | tf_op jit(solution)/shard_map/while/body/eval_jaxpr/dot_general | solution.py:113
  372.1 4.8 %fusion.173 = f32[3,512]{1,0:T(4,128)S(1)} fusion(f32[2560]{0:T(1024)S(1)} %get-tuple-element.531, f32[512]{0:T(512)S(1)} %bitcast.237, f32[2560]{0:T(1024)S(1)} %get-tuple-element.533, f32[512]{0:T(512)S(1)} %bitcast.238, f32[2560]{0:T(1024)S(1)} %get-tuple-element.535, f32[512]{0:T(512)S(1)} %bitcast.236, ...), kind=kOutput, calls=%fused_computation.119.clone.1 | convolution fusion | flops 62917632 | bytes 98821 | tf_op jit(solution)/shard_map/while/body/eval_jaxpr/dot_general | solution.py:113
  378.4 4.8 %fusion.173 = f32[3,512]{1,0:T(4,128)S(1)} fusion(f32[2560]{0:T(1024)S(1)} %get-tuple-element.531, f32[512]{0:T(512)S(1)} %bitcast.237, f32[2560]{0:T(1024)S(1)} %get-tuple-element.533, f32[512]{0:T(512)S(1)} %bitcast.238, f32[2560]{0:T(1024)S(1)} %get-tuple-element.535, f32[512]{0:T(512)S(1)} %bitcast.236, ...), kind=kOutput, calls=%fused_computation.119.clone.1 | convolution fusion | flops 62917632 | bytes 98821 | tf_op jit(solution)/shard_map/while/body/eval_jaxpr/dot_general | solution.py:113
  384.8 4.8 %fusion.173 = f32[3,512]{1,0:T(4,128)S(1)} fusion(f32[2560]{0:T(1024)S(1)} %get-tuple-element.531, f32[512]{0:T(512)S(1)} %bitcast.237, f32[2560]{0:T(1024)S(1)} %get-tuple-element.533, f32[512]{0:T(512)S(1)} %bitcast.238, f32[2560]{0:T(1024)S(1)} %get-tuple-element.535, f32[512]{0:T(512)S(1)} %bitcast.236, ...), kind=kOutput, calls=%fused_computation.119.clone.1 | convolution fusion | flops 62917632 | bytes 98821 | tf_op jit(solution)/shard_map/while/body/eval_jaxpr/dot_general | solution.py:113
  391.1 4.8 %fusion.173 = f32[3,512]{1,0:T(4,128)S(1)} fusion(f32[2560]{0:T(1024)S(1)} %get-tuple-element.531, f32[512]{0:T(512)S(1)} %bitcast.237, f32[2560]{0:T(1024)S(1)} %get-tuple-element.533, f32[512]{0:T(512)S(1)} %bitcast.238, f32[2560]{0:T(1024)S(1)} %get-tuple-element.535, f32[512]{0:T(512)S(1)} %bitcast.236, ...), kind=kOutput, calls=%fused_computation.119.clone.1 | convolution fusion | flops 62917632 | bytes 98821 | tf_op jit(solution)/shard_map/while/body/eval_jaxpr/dot_general | solution.py:113
  397.4 4.8 %fusion.173 = f32[3,512]{1,0:T(4,128)S(1)} fusion(f32[2560]{0:T(1024)S(1)} %get-tuple-element.531, f32[512]{0:T(512)S(1)} %bitcast.237, f32[2560]{0:T(1024)S(1)} %get-tuple-element.533, f32[512]{0:T(512)S(1)} %bitcast.238, f32[2560]{0:T(1024)S(1)} %get-tuple-element.535, f32[512]{0:T(512)S(1)} %bitcast.236, ...), kind=kOutput, calls=%fused_computation.119.clone.1 | convolution fusion | flops 62917632 | bytes 98821 | tf_op jit(solution)/shard_map/while/body/eval_jaxpr/dot_general | solution.py:113
  (174 shorter events, 87.7 us)
Async XLA Ops:
  46.4 7.8 %all-to-all-start = ((f32[4,6,640]{2,1,0:T(8,128)}), f32[4,6,640]{2,1,0:T(8,128)S(1)}, u32[]{:S(2)}, u32[]{:S(2)}) async-start(f32[4,6,640]{2,1,0:T(8,128)} %broadcast_in_dim.18), calls=%async_computation | async-start | bytes 163840 | tf_op jit(solution)/shard_map/all_to_all | solution.py:23
  54.2 11.9 %collective-permute-start = (f32[6,2560]{1,0:T(8,128)S(1)}, f32[6,2560]{1,0:T(8,128)S(1)}, u32[]{:S(2)}, u32[]{:S(2)}) collective-permute-start(f32[6,2560]{1,0:T(8,128)S(1)} %bitcast.226), channel_id=1, source_target_pairs={{0,8},{4,12},{8,16},{12,20},{16,24},{20,28},{24,32},{28,36},{32,40... | collective-permute-start | bytes 184328 | tf_op jit(solution)/shard_map/ppermute | solution.py:40
  56.5 9.6 %collective-permute-start.1 = (f32[6,2560]{1,0:T(8,128)S(1)}, f32[6,2560]{1,0:T(8,128)S(1)}, u32[]{:S(2)}, u32[]{:S(2)}) collective-permute-start(f32[6,2560]{1,0:T(8,128)S(1)} %bitcast.227), channel_id=1, source_target_pairs={{0,4},{4,8},{8,12},{12,16},{16,20},{20,24},{24,28},{28,32},{32,36}... | collective-permute-start | bytes 184328 | tf_op jit(solution)/shard_map/ppermute | solution.py:40
  62.9 5.8 %collective-permute-start.2 = (f32[6,2560]{1,0:T(8,128)S(1)}, f32[6,2560]{1,0:T(8,128)S(1)}, u32[]{:S(2)}, u32[]{:S(2)}) collective-permute-start(f32[6,2560]{1,0:T(8,128)S(1)} %bitcast.228), channel_id=1, source_target_pairs={{4,0},{8,4},{12,8},{16,12},{20,16},{24,20},{28,24},{32,28},{36,32}... | collective-permute-start | bytes 184328 | tf_op jit(solution)/shard_map/ppermute | solution.py:40
  64.8 5.8 %collective-permute-start.3 = (f32[6,2560]{1,0:T(8,128)S(1)}, f32[6,2560]{1,0:T(8,128)S(1)}, u32[]{:S(2)}, u32[]{:S(2)}) collective-permute-start(f32[6,2560]{1,0:T(8,128)S(1)} %bitcast.229), channel_id=1, source_target_pairs={{8,0},{12,4},{16,8},{20,12},{24,16},{28,20},{32,24},{36,28},{40,32... | collective-permute-start | bytes 184328 | tf_op jit(solution)/shard_map/ppermute | solution.py:40
  66.2 4.5 %copy-start = (f32[3,640]{1,0:T(4,128)S(1)}, f32[3,640]{1,0:T(4,128)}, u32[]{:S(2)}) copy-start(f32[3,640]{1,0:T(4,128)} %param.12) | copy-start | bytes 23044
  70.7 68.6 %copy-start.1 = (f32[3,640]{1,0:T(4,128)S(1)}, f32[3,640]{1,0:T(4,128)}, u32[]{:S(2)}) copy-start(f32[3,640]{1,0:T(4,128)} %param.13) | copy-start | bytes 23044
  70.7 72.6 %copy-start.2 = (f32[3,512]{1,0:T(4,128)S(1)}, f32[3,512]{1,0:T(4,128)}, u32[]{:S(2)}) copy-start(f32[3,512]{1,0:T(4,128)} %param.14) | copy-start | bytes 18436
  140.0 7.8 %all-to-all-start.1 = ((f32[4,6,640]{2,1,0:T(8,128)}), f32[4,6,640]{2,1,0:T(8,128)S(1)}, u32[]{:S(2)}, u32[]{:S(2)}) async-start(f32[4,6,640]{2,1,0:T(8,128)} %broadcast_in_dim.19), calls=%async_computation.1 | async-start | bytes 163840 | tf_op jit(solution)/shard_map/all_to_all | solution.py:23
  147.8 11.4 %collective-permute-start.4 = (f32[6,2560]{1,0:T(8,128)S(1)}, f32[6,2560]{1,0:T(8,128)S(1)}, u32[]{:S(2)}, u32[]{:S(2)}) collective-permute-start(f32[6,2560]{1,0:T(8,128)S(1)} %bitcast.214), channel_id=1, source_target_pairs={{0,8},{4,12},{8,16},{12,20},{16,24},{20,28},{24,32},{28,36},{32,40... | collective-permute-start | bytes 184328 | tf_op jit(solution)/shard_map/ppermute | solution.py:40
  149.3 9.9 %collective-permute-start.5 = (f32[6,2560]{1,0:T(8,128)S(1)}, f32[6,2560]{1,0:T(8,128)S(1)}, u32[]{:S(2)}, u32[]{:S(2)}) collective-permute-start(f32[6,2560]{1,0:T(8,128)S(1)} %bitcast.215), channel_id=1, source_target_pairs={{0,4},{4,8},{8,12},{12,16},{16,20},{20,24},{24,28},{28,32},{32,36}... | collective-permute-start | bytes 184328 | tf_op jit(solution)/shard_map/ppermute | solution.py:40
  155.8 5.8 %collective-permute-start.6 = (f32[6,2560]{1,0:T(8,128)S(1)}, f32[6,2560]{1,0:T(8,128)S(1)}, u32[]{:S(2)}, u32[]{:S(2)}) collective-permute-start(f32[6,2560]{1,0:T(8,128)S(1)} %bitcast.216), channel_id=1, source_target_pairs={{4,0},{8,4},{12,8},{16,12},{20,16},{24,20},{28,24},{32,28},{36,32}... | collective-permute-start | bytes 184328 | tf_op jit(solution)/shard_map/ppermute | solution.py:40
  157.7 5.8 %collective-permute-start.7 = (f32[6,2560]{1,0:T(8,128)S(1)}, f32[6,2560]{1,0:T(8,128)S(1)}, u32[]{:S(2)}, u32[]{:S(2)}) collective-permute-start(f32[6,2560]{1,0:T(8,128)S(1)} %bitcast.217), channel_id=1, source_target_pairs={{8,0},{12,4},{16,8},{20,12},{24,16},{28,20},{32,24},{36,28},{40,32... | collective-permute-start | bytes 184328 | tf_op jit(solution)/shard_map/ppermute | solution.py:40
  233.0 7.8 %all-to-all-start.2 = ((f32[4,6,640]{2,1,0:T(8,128)}), f32[4,6,640]{2,1,0:T(8,128)S(1)}, u32[]{:S(2)}, u32[]{:S(2)}) async-start(f32[4,6,640]{2,1,0:T(8,128)} %broadcast_in_dim.20), calls=%async_computation.2 | async-start | bytes 163840 | tf_op jit(solution)/shard_map/all_to_all | solution.py:23
  240.8 11.3 %collective-permute-start.8 = (f32[6,2560]{1,0:T(8,128)S(1)}, f32[6,2560]{1,0:T(8,128)S(1)}, u32[]{:S(2)}, u32[]{:S(2)}) collective-permute-start(f32[6,2560]{1,0:T(8,128)S(1)} %bitcast.231), channel_id=1, source_target_pairs={{0,8},{4,12},{8,16},{12,20},{16,24},{20,28},{24,32},{28,36},{32,40... | collective-permute-start | bytes 184328 | tf_op jit(solution)/shard_map/ppermute | solution.py:40
  242.2 9.9 %collective-permute-start.9 = (f32[6,2560]{1,0:T(8,128)S(1)}, f32[6,2560]{1,0:T(8,128)S(1)}, u32[]{:S(2)}, u32[]{:S(2)}) collective-permute-start(f32[6,2560]{1,0:T(8,128)S(1)} %bitcast.232), channel_id=1, source_target_pairs={{0,4},{4,8},{8,12},{12,16},{16,20},{20,24},{24,28},{28,32},{32,36}... | collective-permute-start | bytes 184328 | tf_op jit(solution)/shard_map/ppermute | solution.py:40
  248.6 5.8 %collective-permute-start.10 = (f32[6,2560]{1,0:T(8,128)S(1)}, f32[6,2560]{1,0:T(8,128)S(1)}, u32[]{:S(2)}, u32[]{:S(2)}) collective-permute-start(f32[6,2560]{1,0:T(8,128)S(1)} %bitcast.233), channel_id=1, source_target_pairs={{4,0},{8,4},{12,8},{16,12},{20,16},{24,20},{28,24},{32,28},{36,32}... | collective-permute-start | bytes 184328 | tf_op jit(solution)/shard_map/ppermute | solution.py:40
  250.6 5.8 %collective-permute-start.11 = (f32[6,2560]{1,0:T(8,128)S(1)}, f32[6,2560]{1,0:T(8,128)S(1)}, u32[]{:S(2)}, u32[]{:S(2)}) collective-permute-start(f32[6,2560]{1,0:T(8,128)S(1)} %bitcast.234), channel_id=1, source_target_pairs={{8,0},{12,4},{16,8},{20,12},{24,16},{28,20},{32,24},{36,28},{40,32... | collective-permute-start | bytes 184328 | tf_op jit(solution)/shard_map/ppermute | solution.py:40
  326.9 26.0 %copy-start.4 = (f32[3,640]{1,0:T(4,128)}, f32[3,640]{1,0:T(4,128)S(1)}, u32[]{:S(2)}) copy-start(f32[3,640]{1,0:T(4,128)S(1)} %multiply_add_fusion) | copy-start | bytes 23044
  327.6 7.8 %all-to-all-start.3 = ((f32[4,6,640]{2,1,0:T(8,128)}), f32[4,6,640]{2,1,0:T(8,128)S(1)}, u32[]{:S(2)}, u32[]{:S(2)}) async-start(f32[4,6,640]{2,1,0:T(8,128)} %broadcast_in_dim.22), calls=%async_computation.3 | async-start | bytes 163840 | tf_op jit(solution)/shard_map/all_to_all | solution.py:23
  335.4 13.0 %collective-permute-start.12 = (f32[6,2560]{1,0:T(8,128)S(1)}, f32[6,2560]{1,0:T(8,128)S(1)}, u32[]{:S(2)}, u32[]{:S(2)}) collective-permute-start(f32[6,2560]{1,0:T(8,128)S(1)} %bitcast.219), channel_id=1, source_target_pairs={{0,12},{4,16},{8,20},{12,24},{16,28},{20,32},{24,36},{28,40},{32,4... | collective-permute-start | bytes 184328 | tf_op jit(solution)/shard_map/ppermute | solution.py:40
  340.7 61.5 %copy-start.5 = (f32[3,4]{1,0:T(4,128)}, f32[3,4]{1,0:T(4,128)S(1)}, u32[]{:S(2)}) copy-start(f32[3,4]{1,0:T(4,128)S(1)} %multiply_add_fusion.7) | copy-start | bytes 148
  340.7 9.2 %collective-permute-start.13 = (f32[6,2560]{1,0:T(8,128)S(1)}, f32[6,2560]{1,0:T(8,128)S(1)}, u32[]{:S(2)}, u32[]{:S(2)}) collective-permute-start(f32[6,2560]{1,0:T(8,128)S(1)} %bitcast.220), channel_id=1, source_target_pairs={{0,8},{4,12},{8,16},{12,20},{16,24},{20,28},{24,32},{28,36},{32,40... | collective-permute-start | bytes 184328 | tf_op jit(solution)/shard_map/ppermute | solution.py:40
  342.0 8.0 %collective-permute-start.14 = (f32[6,2560]{1,0:T(8,128)S(1)}, f32[6,2560]{1,0:T(8,128)S(1)}, u32[]{:S(2)}, u32[]{:S(2)}) collective-permute-start(f32[6,2560]{1,0:T(8,128)S(1)} %bitcast.221), channel_id=1, source_target_pairs={{0,4},{4,8},{8,12},{12,16},{16,20},{20,24},{24,28},{28,32},{32,36}... | collective-permute-start | bytes 184328 | tf_op jit(solution)/shard_map/ppermute | solution.py:40
  345.1 5.8 %collective-permute-start.15 = (f32[6,2560]{1,0:T(8,128)S(1)}, f32[6,2560]{1,0:T(8,128)S(1)}, u32[]{:S(2)}, u32[]{:S(2)}) collective-permute-start(f32[6,2560]{1,0:T(8,128)S(1)} %bitcast.222), channel_id=1, source_target_pairs={{4,0},{8,4},{12,8},{16,12},{20,16},{24,20},{28,24},{32,28},{36,32}... | collective-permute-start | bytes 184328 | tf_op jit(solution)/shard_map/ppermute | solution.py:40
  347.1 5.8 %collective-permute-start.16 = (f32[6,2560]{1,0:T(8,128)S(1)}, f32[6,2560]{1,0:T(8,128)S(1)}, u32[]{:S(2)}, u32[]{:S(2)}) collective-permute-start(f32[6,2560]{1,0:T(8,128)S(1)} %bitcast.223), channel_id=1, source_target_pairs={{8,0},{12,4},{16,8},{20,12},{24,16},{28,20},{32,24},{36,28},{40,32... | collective-permute-start | bytes 184328 | tf_op jit(solution)/shard_map/ppermute | solution.py:40
  348.4 8.9 %collective-permute-start.17 = (f32[6,2560]{1,0:T(8,128)S(1)}, f32[6,2560]{1,0:T(8,128)S(1)}, u32[]{:S(2)}, u32[]{:S(2)}) collective-permute-start(f32[6,2560]{1,0:T(8,128)S(1)} %bitcast.224), channel_id=1, source_target_pairs={{12,0},{16,4},{20,8},{24,12},{28,16},{32,20},{36,24},{40,28},{44,3... | collective-permute-start | bytes 184328 | tf_op jit(solution)/shard_map/ppermute | solution.py:40
  357.3 0.7 copy-start.3
where the time goes:
time: 408 us; the launch traced here: 403 us
  blocking collectives  159 us (39%)
  matrix products  124 us (30%)
  starting transfers between devices  60.9 us (15%)
  waiting for transfers between devices  37.1 us (9%)
  local copies, waits for them, and re-layouts  10.8 us (3%)
  other arithmetic  9.22 us (2%)
    psum x16, blocking collectives, over_axes(): return functools.reduce(lax.psum, axes, x)  159 us
    dot_general x22, matrix products, add_slab(): jnp.dot(values, tile, precision=precise, preferred_element_type=jnp.float32)  121 us
    ppermute x18, starting transfers between devices, from_behind(): lax.ppermute(value, axis, [(source, source + steps) for source in range(i...  47.7 us
    ppermute x18, waiting for transfers between devices, from_behind(): lax.ppermute(value, axis, [(source, source + steps) for source in range(i...  20.1 us
    all_to_all x4, waiting for transfers between devices, copy_for_each(): return lax.all_to_all(copies, axis, split_axis=0, concat_axis=0, tiled=True)  17 us
    all_to_all x4, starting transfers between devices, copy_for_each(): return lax.all_to_all(copies, axis, split_axis=0, concat_axis=0, tiled=True)  13.2 us
  transfers between devices with their start and end apart: 22, of which 13 were waited for; matrix products, arithmetic and copies ran while one was open for 1% of the time, Pallas kernels for 0%

commit v1 on v0

v1 whole, which is shorter than its diff:
```python
import functools
import math

import jax
import jax.numpy as jnp
from jax import lax
from jax.experimental import pallas as pl
from jax.experimental.pallas import tpu as pltpu
from jax.sharding import PartitionSpec as P

MESH = pl.DeviceIdType.MESH
ITERS = 3
REACH = 2
FAR = REACH + 1
NB = 64
NG = 4
RING = 16
OWN = 640
TGT = 512
LANE = 128
CH = OWN // LANE
SLAB = OWN * NG
NSRC = SLAB * NB
STRETCH = 4.0 * SLAB
SHIFT = 2.0
TINY = 1e-6
LOG2E = 1.4426950408889634
XSCALE = math.sqrt(0.6 * LOG2E)
YZ = -STRETCH * LOG2E
ROOT = 1.0 / math.sqrt(NSRC)
NEAR_SLOTS = (2 * REACH + 1) * NG
FAR_SLOTS = (2 * FAR + 1) * NG
SUB = 64
f32 = jnp.float32
bf16 = jnp.bfloat16
HIGH = lax.Precision.HIGHEST


def split(v):
    hi = v.astype(bf16)
    return hi, (v - hi.astype(f32)).astype(bf16)


def least_squares(hessenberg, beta):
    count = len(hessenberg)
    right_side = [beta] + [jnp.zeros_like(beta) for k in range(count)]
    upper = []
    cosines = []
    sines = []
    for k in range(count):
        column = list(hessenberg[k])
        for i in range(k):
            top = cosines[i] * column[i] + sines[i] * column[i + 1]
            lower = -sines[i] * column[i] + cosines[i] * column[i + 1]
            column[i] = top
            column[i + 1] = lower
        radius = jnp.sqrt(column[k] * column[k] + column[k + 1] * column[k + 1])
        cosine = column[k] / radius
        sine = column[k + 1] / radius
        column[k] = radius
        cosines.append(cosine)
        sines.append(sine)
        right_side[k + 1] = -sine * right_side[k]
        right_side[k] = cosine * right_side[k]
        upper.append(column[: k + 1])
    solved = [None] * count
    for k in reversed(range(count)):
        running = right_side[k]
        for j in range(k + 1, count):
            running = running - upper[j][k] * solved[j]
        solved[k] = running / upper[k][k]
    return solved


def basis_rows(x, y, z):
    return (
        jnp.full_like(x, ROOT),
        (2.0 * x / NB - 1.0) * ROOT,
        (2.0 * y - 1.0) * ROOT,
        (2.0 * z - 1.0) * ROOT,
    )


def coefficients(gram):
    lane = lax.broadcasted_iota(jnp.int32, (8, LANE), 1)
    row = lax.broadcasted_iota(jnp.int32, (8, LANE), 0)
    tail_lanes = (lane >= 12) & (lane < 16)

    def total(v):
        return jnp.sum(v, axis=1, keepdims=True)

    def times_gram(v):
        return jnp.dot(v, gram, precision=HIGH, preferred_element_type=f32)

    def shifted(v):
        up = pltpu.roll(v, 3, 1)
        across = pltpu.roll(v, 4, 1)
        moved = jnp.where(lane < 12, up, jnp.where((lane >= 16) & (lane < 20), across, 0.0))
        moved = jnp.where(lane < 3, 0.0, moved)
        return moved + SHIFT * v

    first = jnp.where((lane == row) & (row < 3), 1.0, 0.0)
    first_gram = times_gram(first)
    beta = jnp.sqrt(total(first_gram * first) + TINY)
    heads = [first / beta]
    tails = [jnp.zeros_like(first)]
    grams = [first_gram / beta]
    hessenberg = []
    for k in range(ITERS):
        head = shifted(heads[k]) + tails[k]
        tail = jnp.where(tail_lanes, grams[k], 0.0)
        head_gram = times_gram(head)
        column = [
            total(head_gram * heads[i]) + total(tail * tails[i]) for i in range(k + 1)
        ]
        for i in range(k + 1):
            head = head - column[i] * heads[i]
            tail = tail - column[i] * tails[i]
        rest_gram = times_gram(head)
        length = jnp.sqrt(total(rest_gram * head) + total(tail * tail) + TINY)
        column.append(length)
        hessenberg.append(column)
        heads.append(head / length)
        tails.append(tail / length)
        grams.append(rest_gram / length)
    solved = least_squares(hessenberg, beta)
    head = solved[0] * heads[0]
    tail = solved[0] * tails[0]
    for k in range(1, ITERS):
        head = head + solved[k] * heads[k]
        tail = tail + solved[k] * tails[k]
    return head, tail


def kernel(
    coords_ref,
    values_ref,
    tcoords_ref,
    owner_ref,
    weights_ref,
    poly_ref,
    mapped_ref,
    c0,
    f1,
    f2,
    kh,
    kl,
    th,
    tl,
    cb,
    rows,
    trows,
    fmat,
    mmat,
    ga,
    gb,
    send_sem,
    recv_sem,
    a_send,
    a_recv,
    b_send,
    b_recv,
):
    p = lax.axis_index("blk")
    g = lax.axis_index("grp")
    xi = p // RING
    zi = p % RING
    own = FAR * NG + g

    def valid(o):
        return (p + o >= 0) & (p + o < NB)

    halo = []
    for d in range(1, NG):
        halo.append((0, (g + d) % NG))
    for dist in range(1, FAR + 1):
        for o in (dist, -dist):
            for d in range(NG):
                halo.append((o, (g + d) % NG))
    ring_a = [(xi * RING + (zi + d) % RING, g) for d in range(1, RING)]
    ring_b = [
        (((xi + dx) % 4) * RING + zi, (g + dg) % NG)
        for dx in range(4)
        for dg in range(NG)
        if (dx, dg) != (0, 0)
    ]

    barrier = pltpu.get_barrier_semaphore()

    def signal(q, h):
        pl.semaphore_signal(barrier, inc=1, device_id=(q, h), device_id_type=MESH)

    expected = NG - 1 + len(ring_a) + len(ring_b)
    for o, h in halo:
        if o == 0:
            signal(p, h)
        else:
            pl.when(valid(o))(functools.partial(signal, p + o, h))
    for o in range(-FAR, FAR + 1):
        if o != 0:
            expected = expected + jnp.where(valid(o), NG, 0)
    for q, h in ring_a + ring_b:
        signal(q, h)

    for t in range(CH):
        lanes = slice(t * LANE, (t + 1) * LANE)
        c0[own, 3 * t : 3 * t + 3, :] = coords_ref[:, lanes]
        c0[own, 16 + 3 * t : 16 + 3 * t + 3, :] = values_ref[:, lanes]
    base = p.astype(f32)
    sx, sy, sz = coords_ref[0:1, :], coords_ref[1:2, :], coords_ref[2:3, :]
    rows[0:1, :] = (sx - base) * XSCALE
    rows[1:2, :] = sy
    rows[2:3, :] = sz
    fmat[...] = jnp.zeros_like(fmat)
    mmat[...] = jnp.zeros_like(mmat)
    fmat[0:3, :] = values_ref[...]
    for i, part in enumerate(basis_rows(sx, sy, sz)):
        fmat[12 + i : 13 + i, :] = part
    tx, ty, tz = tcoords_ref[0:1, :], tcoords_ref[1:2, :], tcoords_ref[2:3, :]
    owner = owner_ref[...]
    for o in range(-FAR, FAR + 1):
        inside = jnp.abs(owner - (p + o)) <= REACH
        trows[FAR + o] = jnp.where(inside, (tx - base) * XSCALE, 1e6)
    trows[7] = ty
    trows[8] = tz
    for i, part in enumerate(basis_rows(tx, ty, tz)):
        mmat[24 + i : 25 + i, :] = part

    absent = jnp.where(
        lax.broadcasted_iota(jnp.int32, (32, LANE), 0) % 3 == 0, 1e5, 0.0
    )
    absent = jnp.where(lax.broadcasted_iota(jnp.int32, (32, LANE), 0) < 15, absent, 0.0)
    for o in range(-FAR, FAR + 1):
        if o != 0:

            @pl.when(jnp.logical_not(valid(o)))
            def _():
                for h in range(NG):
                    slot = (FAR + o) * NG + h
                    c0[slot] = absent
                    f1[slot] = jnp.zeros((16, LANE), f32)
                    f2[slot] = jnp.zeros((16, LANE), f32)

    pl.semaphore_wait(barrier, expected)

    def block_copy(buf, which, o, h):
        return pltpu.make_async_remote_copy(
            src_ref=buf.at[own],
            dst_ref=buf.at[(FAR - o) * NG + g],
            send_sem=send_sem.at[which, (FAR + o) * NG + h],
            recv_sem=recv_sem.at[which, (FAR - o) * NG + g],
            device_id=(p + o, h),
            device_id_type=MESH,
        )

    def send_all(buf, which):
        for o, h in halo:
            copy = block_copy(buf, which, o, h)
            if o == 0:
                copy.start()
            else:
                pl.when(valid(o))(copy.start)

    def wait_send_all(buf, which):
        for o, h in halo:
            copy = block_copy(buf, which, o, h)
            if o == 0:
                copy.wait_send()
            else:
                pl.when(valid(o))(copy.wait_send)

    def wait_block(buf, which, o, h):
        slot = (FAR + o) * NG + h
        pltpu.make_async_remote_copy(
            src_ref=buf.at[own],
            dst_ref=buf.at[slot],
            send_sem=send_sem.at[which, slot],
            recv_sem=recv_sem.at[which, slot],
            device_id=(p + o, h),
            device_id_type=MESH,
        ).wait_recv()

    def place(k):
        oi = k // NG
        dist = (oi + 1) // 2
        o = jnp.where(oi % 2 == 1, dist, -dist)
        h = (g + k % NG) % NG
        return o, h, (FAR + o) * NG + h

    send_all(c0, 0)

    def column_coords(slot, t):
        cc = c0[slot, 3 * t : 3 * t + 3, :]
        sides = []
        for i in range(3):
            row = cc[i : i + 1, :]
            if i == 0:
                row = (row - base) * XSCALE
            sides.append(jnp.broadcast_to(row, (LANE, LANE)).T)
        for i in range(3):
            cb[t, i] = sides[i]

    def tile(t, sub, rx, ry, rz):
        at = slice(sub * SUB, (sub + 1) * SUB)
        dx = cb[t, 0, at, :] - rx
        dy = cb[t, 1, at, :] - ry
        dz = cb[t, 2, at, :] - rz
        return jnp.exp2(YZ * (dy * dy + dz * dz) - dx * dx)

    def near_values(slot, t):
        cc = c0[slot, 3 * t : 3 * t + 3, :]
        parts = [c0[slot, 16 + 3 * t : 16 + 3 * t + 3, :]]
        parts += basis_rows(cc[0:1], cc[1:2], cc[2:3])
        parts.append(jnp.zeros((1, LANE), f32))
        return jnp.concatenate(split(jnp.concatenate(parts, axis=0)), axis=0)

    def build(k, acc):
        o, h, slot = place(k)

        @pl.when((k > 0) & valid(o))
        def _():
            wait_block(c0, 0, o, h)

        start = pl.multiple_of(k * OWN, OWN)
        for t in range(CH):
            column_coords(slot, t)
        for t in range(CH):
            for n in range(OWN // LANE):
                lanes = slice(n * LANE, (n + 1) * LANE)
                rx, ry, rz = rows[0:1, lanes], rows[1:2, lanes], rows[2:3, lanes]
                for sub in range(LANE // SUB):
                    hi, lo = split(tile(t, sub, rx, ry, rz))
                    at = pl.ds(start + t * LANE + sub * SUB, SUB)
                    kh[at, lanes] = hi
                    kl[at, lanes] = lo
            v = near_values(slot, t)
            at = pl.ds(start + t * LANE, LANE)
            acc = acc + jnp.dot(v, kh[at, :], preferred_element_type=f32)
            acc = acc + jnp.dot(v, kl[at, :], preferred_element_type=f32)
        return acc

    acc = lax.fori_loop(0, NEAR_SLOTS, build, jnp.zeros((16, OWN), f32))
    image = acc[0:8] + acc[8:16]
    first = image[0:3] - SHIFT * fmat[0:3, :]
    fmat[3:6, :] = first
    fmat[16:20, :] = image[3:7] - SHIFT * fmat[12:16, :]

    def keep_own(buf, v):
        for t in range(CH):
            buf[own, 3 * t : 3 * t + 3, :] = v[:, t * LANE : (t + 1) * LANE]

    keep_own(f1, first)
    send_all(f1, 1)

    def padded_split(v):
        v = jnp.concatenate([v, jnp.zeros((5, LANE), f32)], axis=0)
        return jnp.concatenate(split(v), axis=0)

    def apply_near(buf, which):
        def step(k, acc):
            o, h, slot = place(k)

            @pl.when((k > 0) & valid(o))
            def _():
                wait_block(buf, which, o, h)

            start = pl.multiple_of(k * OWN, OWN)
            v = jnp.concatenate(
                [padded_split(buf[slot, 3 * t : 3 * t + 3, :]) for t in range(CH)], axis=1
            )
            at = pl.ds(start, OWN)
            acc = acc + jnp.dot(v, kh[at, :], preferred_element_type=f32)
            return acc + jnp.dot(v, kl[at, :], preferred_element_type=f32)

        acc = lax.fori_loop(0, NEAR_SLOTS, step, jnp.zeros((16, OWN), f32))
        return acc[0:3] + acc[8:11]

    second = apply_near(f1, 1) - SHIFT * first
    fmat[6:9, :] = second
    keep_own(f2, second)
    send_all(f2, 2)
    third = apply_near(f2, 2) - SHIFT * second
    fmat[9:12, :] = third

    everything = fmat[...]
    ga[zi] = lax.dot_general(
        fmat[0:24, :],
        everything,
        (((1,), (1,)), ((), ())),
        precision=HIGH,
        preferred_element_type=f32,
    )

    def a_copy(d):
        q, h = ring_a[d - 1]
        return pltpu.make_async_remote_copy(
            src_ref=ga.at[zi],
            dst_ref=ga.at[zi],
            send_sem=a_send.at[d],
            recv_sem=a_recv.at[zi],
            device_id=(q, h),
            device_id_type=MESH,
        )

    def a_wait(d):
        slot = (zi + d) % RING
        pltpu.make_async_remote_copy(
            src_ref=ga.at[zi],
            dst_ref=ga.at[slot],
            send_sem=a_send.at[d],
            recv_sem=a_recv.at[slot],
            device_id=ring_a[d - 1],
            device_id_type=MESH,
        ).wait_recv()

    me_b = xi * NG + g

    def b_copy(i):
        return pltpu.make_async_remote_copy(
            src_ref=gb.at[me_b],
            dst_ref=gb.at[me_b],
            send_sem=b_send.at[i],
            recv_sem=b_recv.at[me_b],
            device_id=ring_b[i],
            device_id_type=MESH,
        )

    def b_wait(i):
        dx, dg = (i + 1) // NG, (i + 1) % NG
        slot = ((xi + dx) % 4) * NG + (g + dg) % NG
        pltpu.make_async_remote_copy(
            src_ref=gb.at[me_b],
            dst_ref=gb.at[slot],
            send_sem=b_send.at[i],
            recv_sem=b_recv.at[slot],
            device_id=ring_b[i],
            device_id_type=MESH,
        ).wait_recv()

    for d in range(1, RING):
        a_copy(d).start()

    def far_values(slot, t):
        cc = c0[slot, 3 * t : 3 * t + 3, :]
        parts = [
            c0[slot, 16 + 3 * t : 16 + 3 * t + 3, :],
            f1[slot, 3 * t : 3 * t + 3, :],
            f2[slot, 3 * t : 3 * t + 3, :],
            jnp.zeros((3, LANE), f32),
        ]
        parts += basis_rows(cc[0:1], cc[1:2], cc[2:3])
        return jnp.concatenate(split(jnp.concatenate(parts, axis=0)), axis=0)

    def target(k, acc):
        o, h, slot = place(k)

        @pl.when((k >= NEAR_SLOTS) & valid(o))
        def _():
            wait_block(c0, 0, o, h)
            wait_block(f1, 1, o, h)
            wait_block(f2, 2, o, h)

        for t in range(CH):
            column_coords(slot, t)
        for t in range(CH):
            for n in range(TGT // LANE):
                lanes = slice(n * LANE, (n + 1) * LANE)
                rx = trows[FAR + o, :, lanes]
                ry, rz = trows[7, :, lanes], trows[8, :, lanes]
                for sub in range(LANE // SUB):
                    hi, lo = split(tile(t, sub, rx, ry, rz))
                    at = slice(t * LANE + sub * SUB, t * LANE + (sub + 1) * SUB)
                    th[at, lanes] = hi
                    tl[at, lanes] = lo
            v = far_values(slot, t)
            at = slice(t * LANE, (t + 1) * LANE)
            acc = acc + jnp.dot(v, th[at, :], preferred_element_type=f32)
            acc = acc + jnp.dot(v, tl[at, :], preferred_element_type=f32)
        return acc

    half = FAR_SLOTS // 2
    acc = lax.fori_loop(0, half, target, jnp.zeros((32, TGT), f32))

    for d in range(1, RING):
        a_wait(d)
    part = ga[0]
    for i in range(1, RING):
        part = part + ga[i]
    gb[me_b] = part
    for i in range(RING - 1):
        b_copy(i).start()

    acc = lax.fori_loop(half, FAR_SLOTS, target, acc)
    mmat[0:16, :] = acc[0:16] + acc[16:32]

    for i in range(RING - 1):
        b_wait(i)
    whole = gb[0]
    for i in range(1, RING):
        whole = whole + gb[i]
    gram = jnp.concatenate([whole, jnp.zeros((LANE - 24, LANE), f32)], axis=0)
    head, tail = coefficients(gram)
    weights = jnp.dot(head, everything, precision=HIGH, preferred_element_type=f32)
    weights_ref[...] = weights[0:3]
    poly_ref[...] = pltpu.roll(tail, LANE - 12, 1)[0:3, 0:4]
    both = head + pltpu.roll(tail, 12, 1)
    mapped = jnp.dot(both, mmat[...], precision=HIGH, preferred_element_type=f32)
    mapped_ref[...] = mapped[0:3]

    wait_send_all(c0, 0)
    wait_send_all(f1, 1)
    wait_send_all(f2, 2)
    for d in range(1, RING):
        a_copy(d).wait_send()
    for i in range(RING - 1):
        b_copy(i).wait_send()


def shards(source_coords, source_values, target_coords, target_owner):
    vmem = pl.BlockSpec(memory_space=pltpu.VMEM)
    dma = pltpu.SemaphoreType.DMA
    return pl.pallas_call(
        kernel,
        out_shape=(
            jax.ShapeDtypeStruct((3, OWN), f32),
            jax.ShapeDtypeStruct((3, 4), f32),
            jax.ShapeDtypeStruct((3, TGT), f32),
        ),
        in_specs=[vmem] * 4,
        out_specs=(vmem,) * 3,
        scratch_shapes=[
            pltpu.VMEM((FAR_SLOTS, 32, LANE), f32),
            pltpu.VMEM((FAR_SLOTS, 16, LANE), f32),
            pltpu.VMEM((FAR_SLOTS, 16, LANE), f32),
            pltpu.VMEM((NEAR_SLOTS * OWN, OWN), bf16),
            pltpu.VMEM((NEAR_SLOTS * OWN, OWN), bf16),
            pltpu.VMEM((OWN, TGT), bf16),
            pltpu.VMEM((OWN, TGT), bf16),
            pltpu.VMEM((CH, 3, LANE, LANE), f32),
            pltpu.VMEM((8, OWN), f32),
            pltpu.VMEM((9, 1, TGT), f32),
            pltpu.VMEM((LANE, OWN), f32),
            pltpu.VMEM((LANE, TGT), f32),
            pltpu.VMEM((RING, 24, LANE), f32),
            pltpu.VMEM((RING, 24, LANE), f32),
            dma((3, FAR_SLOTS)),
            dma((3, FAR_SLOTS)),
            dma((RING,)),
            dma((RING,)),
            dma((RING,)),
            dma((RING,)),
        ],
        compiler_params=pltpu.CompilerParams(
            collective_id=0, has_side_effects=True, vmem_limit_bytes=62 * 1024 * 1024
        ),
    )(source_coords, source_values, target_coords, target_owner.reshape(1, TGT))


def solution(mesh):
    both = ("blk", "grp")
    return jax.shard_map(
        shards,
        mesh=mesh,
        in_specs=(P(None, both), P(None, both), P(None, both), P(both)),
        out_specs=(P(None, both), P(), P(None, both)),
        check_vma=False,
    )
```

time: 408 us -> 97.8 us (0.24)
  blocking collectives: 159 us -> 0 us
  matrix products: 124 us -> 0 us
  Pallas kernels: 0 us -> 93.6 us
  starting transfers between devices: 60.9 us -> 0 us
  waiting for transfers between devices: 37.1 us -> 0 us
  other arithmetic: 9.22 us -> 0 us
  local copies, waits for them, and re-layouts: 10.8 us -> 2.49 us
    psum x16 -> x0, blocking collectives: 159 us -> none  [over_axes(): return functools.reduce(lax.psum, axes, x)]
    dot_general x29 -> x0, matrix products: 124 us -> none  [the longest x22 121 us: add_slab(): jnp.dot(values, tile, precision=precise, preferred_element_type=jnp.float32)]
    pallas_call x0 -> x1, Pallas kernels: none -> 93.6 us  [shards(): pl.pallas_call(kernel, out_shape=(jax.ShapeDtypeStruct((3, OWN), f32), ja...]
    ppermute x18 -> x0, starting transfers between devices: 47.7 us -> none  [from_behind(): lax.ppermute(value, axis, [(source, source + steps) for source in range(i...]
    ppermute x18 -> x0, waiting for transfers between devices: 20.1 us -> none  [from_behind(): lax.ppermute(value, axis, [(source, source + steps) for source in range(i...]
    all_to_all x4 -> x0, waiting for transfers between devices: 17 us -> none  [copy_for_each(): return lax.all_to_all(copies, axis, split_axis=0, concat_axis=0, tiled=True)]
    all_to_all x4 -> x0, starting transfers between devices: 13.2 us -> none  [copy_for_each(): return lax.all_to_all(copies, axis, split_axis=0, concat_axis=0, tiled=True)]
    le x7 -> x0, other arithmetic: 4.87 us -> none  [add_slab(): tile = jnp.where((jnp.abs(owners - slab) <= reach)[None, :], tile, 0.0)]
  transfers between devices with their start and end apart: 22 -> 0, of which waited for: 13 -> 0; matrix products, arithmetic and copies ran while one was open for 1% -> 0% of each run, Pallas kernels for 0% -> 0%
where the time goes in v1:
time: 97.8 us; the launch traced here: 96.7 us
  Pallas kernels  93.6 us (96%)
  local copies, waits for them, and re-layouts  2.49 us (3%)
    pallas_call x1, Pallas kernels, shards(): pl.pallas_call(kernel, out_shape=(jax.ShapeDtypeStruct((3, OWN), f32), ja...  93.6 us
    unnamed x7, local copies, waits for them, and re-layouts  2.49 us

profile of v1, /device:TPU:1, one launch (start us, length us, event | category | flops | bytes accessed | tf_op | source)
XLA Modules:
  0.0 96.7 jit_solution(8470598803254672205)
XLA Ops:
  0.6 93.6 %shard_map.67 = (f32[3,640]{1,0:T(4,128)}, f32[3,4]{1,0:T(4,128)}, f32[3,512]{1,0:T(4,128)}) custom-call(f32[3,640]{1,0:T(4,128)} %coords_ref.1, f32[3,640]{1,0:T(4,128)} %values_ref.1, f32[3,512]{1,0:T(4,128)} %tcoords_ref.1, s32[1,512]{1,0:T(1,128)} %bitcast.1), custom_call_target="tpu_custom_call" | custom-call | tf_op jit(solution)/shard_map/pallas_call | solution.py:522
  94.2 0.0 copy-start.1
  94.2 0.0 copy-start
  94.2 1.3 %copy.10 = f32[3,640]{1,0:T(4,128)} copy(f32[3,640]{1,0:T(4,128)} %get-tuple-element.6) | data formatting | bytes 15360
  95.5 0.0 copy-done.1
  95.5 0.6 copy.11
  96.1 0.0 copy-done
  96.1 0.6 copy.12
Async XLA Ops:
  94.2 1.3 %copy-start.1 = (f32[3,4]{1,0:T(4,128)S(1)}, f32[3,4]{1,0:T(4,128)}, u32[]{:S(2)}) copy-start(f32[3,4]{1,0:T(4,128)} %get-tuple-element.7) | copy-start | bytes 148
  94.2 1.9 %copy-start = (f32[3,512]{1,0:T(4,128)S(1)}, f32[3,512]{1,0:T(4,128)}, u32[]{:S(2)}) copy-start(f32[3,512]{1,0:T(4,128)} %get-tuple-element.8) | copy-start | bytes 18436

commit v2 on v1

--- a/solution.py
+++ b/solution.py
@@ -26,11 +26,13 @@
 TINY = 1e-6
 LOG2E = 1.4426950408889634
 XSCALE = math.sqrt(0.6 * LOG2E)
-YZ = -STRETCH * LOG2E
+GRID = math.sqrt(STRETCH * LOG2E / 4.0)
+TERMS = 48
 ROOT = 1.0 / math.sqrt(NSRC)
 NEAR_SLOTS = (2 * REACH + 1) * NG
 FAR_SLOTS = (2 * FAR + 1) * NG
-SUB = 64
+MAGIC = 49152.0
+KEEP = 14
 f32 = jnp.float32
 bf16 = jnp.bfloat16
 HIGH = lax.Precision.HIGHEST
@@ -70,6 +72,47 @@
             running = running - upper[j][k] * solved[j]
         solved[k] = running / upper[k][k]
     return solved
+
+
+def pieces(v, count):
+    out = []
+    for i in range(count):
+        part = v.astype(bf16).astype(f32)
+        out.append(part)
+        v = v - part
+    return out
+
+
+def point_terms(x, y, z, column, extra):
+    one = jnp.ones_like(x)
+    big = 1.0 if column else 8.0
+    fine = []
+    coarse = []
+    scalar = -x * x
+    whole = jnp.zeros_like(x)
+    for v in (y, z):
+        u = (v - 0.5) * GRID
+        n = jnp.floor(u + 0.5)
+        f = u - n
+        f1, f2, f3 = pieces(f, 3)
+        if column:
+            fine += [f1, f2, f3, n, n, n, f1, f1, f2, f2]
+        else:
+            n8 = 8.0 * n
+            fine += [n8, n8, n8, 8.0 * f1, 8.0 * f2, 8.0 * f3, 8.0 * f1, 8.0 * f2, 8.0 * f1, 8.0 * f2]
+        coarse.append(n * big)
+        scalar = scalar - (8.0 * n + 4.0 * f) * f
+        whole = whole - 4.0 * n * n
+    s = pieces(scalar, 3)
+    w = pieces(whole, 2)
+    x1, x2, x3 = pieces(x, 3)
+    if column:
+        fine += s + [one, one, one] + [x1, x1, x2, x2, x1, x3]
+        coarse += w + [one, one, one]
+    else:
+        fine += [one, one, one] + s + [2.0 * v for v in (x1, x2, x1, x2, x3, x1)]
+        coarse += [one, one] + w + [extra]
+    return fine + coarse
 
 
 def basis_rows(x, y, z):
@@ -147,9 +190,12 @@
     kl,
     th,
     tl,
-    cb,
-    rows,
-    trows,
+    acc_near,
+    acc_far,
+    lt,
+    stage,
+    rsrc,
+    rtgt,
     fmat,
     mmat,
     ga,
@@ -208,9 +254,10 @@
         c0[own, 16 + 3 * t : 16 + 3 * t + 3, :] = values_ref[:, lanes]
     base = p.astype(f32)
     sx, sy, sz = coords_ref[0:1, :], coords_ref[1:2, :], coords_ref[2:3, :]
-    rows[0:1, :] = (sx - base) * XSCALE
-    rows[1:2, :] = sy
-    rows[2:3, :] = sz
+    source_terms = point_terms((sx - base) * XSCALE, sy, sz, False, jnp.zeros_like(sx))
+    source_terms += [jnp.zeros_like(sx)] * (TERMS - len(source_terms))
+    rsrc[...] = jnp.concatenate(source_terms, axis=0).astype(bf16)
+    stage[...] = jnp.zeros_like(stage)
     fmat[...] = jnp.zeros_like(fmat)
     mmat[...] = jnp.zeros_like(mmat)
     fmat[0:3, :] = values_ref[...]
@@ -218,11 +265,14 @@
         fmat[12 + i : 13 + i, :] = part
     tx, ty, tz = tcoords_ref[0:1, :], tcoords_ref[1:2, :], tcoords_ref[2:3, :]
     owner = owner_ref[...]
+    target_terms = point_terms((tx - base) * XSCALE, ty, tz, False, jnp.zeros_like(tx))
+    masked = len(target_terms) - 1
+    target_terms += [jnp.zeros_like(tx)] * (TERMS - len(target_terms))
+    target_terms = jnp.concatenate(target_terms, axis=0)
+    at_mask = lax.broadcasted_iota(jnp.int32, (TERMS, TGT), 0) == masked
     for o in range(-FAR, FAR + 1):
-        inside = jnp.abs(owner - (p + o)) <= REACH
-        trows[FAR + o] = jnp.where(inside, (tx - base) * XSCALE, 1e6)
-    trows[7] = ty
-    trows[8] = tz
+        mask = jnp.where(jnp.abs(owner - (p + o)) <= REACH, 0.0, -1e6)
+        rtgt[FAR + o] = jnp.where(at_mask, mask, target_terms).astype(bf16)
     for i, part in enumerate(basis_rows(tx, ty, tz)):
         mmat[24 + i : 25 + i, :] = part
 
@@ -281,31 +331,29 @@
         ).wait_recv()
 
     def place(k):
-        oi = k // NG
-        dist = (oi + 1) // 2
-        o = jnp.where(oi % 2 == 1, dist, -dist)
-        h = (g + k % NG) % NG
+        oi = lax.div(k, NG)
+        dist = lax.div(oi + 1, 2)
+        o = jnp.where(lax.rem(oi, 2) == 1, dist, -dist)
+        h = lax.rem(g + k, NG)
         return o, h, (FAR + o) * NG + h
 
     send_all(c0, 0)
 
-    def column_coords(slot, t):
-        cc = c0[slot, 3 * t : 3 * t + 3, :]
-        sides = []
-        for i in range(3):
-            row = cc[i : i + 1, :]
-            if i == 0:
-                row = (row - base) * XSCALE
-            sides.append(jnp.broadcast_to(row, (LANE, LANE)).T)
-        for i in range(3):
-            cb[t, i] = sides[i]
-
-    def tile(t, sub, rx, ry, rz):
-        at = slice(sub * SUB, (sub + 1) * SUB)
-        dx = cb[t, 0, at, :] - rx
-        dy = cb[t, 1, at, :] - ry
-        dz = cb[t, 2, at, :] - rz
-        return jnp.exp2(YZ * (dy * dy + dz * dz) - dx * dx)
+    def column_terms(slot, k):
+        x, y, z = (c0[slot, pl.ds(i, CH, stride=3), :] for i in range(3))
+        for i, v in enumerate(point_terms((x - base) * XSCALE, y, z, True, None)):
+            stage[pl.ds(i, CH, stride=TERMS), :] = v
+        for t in range(CH):
+            at = pl.ds(pl.multiple_of(k * OWN, OWN) + t * LANE, LANE)
+            lt[at, :] = stage[t * TERMS : (t + 1) * TERMS, :].T.astype(bf16)
+
+    def fill(k, t, right, hi_ref, lo_ref, start):
+        at = pl.ds(pl.multiple_of(k * OWN, OWN) + t * LANE, LANE)
+        put = pl.ds(start + t * LANE, LANE)
+        e = jnp.exp2(jnp.dot(lt[at, :], right, preferred_element_type=f32))
+        hi = (e + MAGIC) - MAGIC
+        hi_ref[put, :] = hi.astype(bf16)
+        lo_ref[put, :] = (e - hi).astype(bf16)
 
     def near_values(slot, t):
         cc = c0[slot, 3 * t : 3 * t + 3, :]
@@ -314,32 +362,41 @@
         parts.append(jnp.zeros((1, LANE), f32))
         return jnp.concatenate(split(jnp.concatenate(parts, axis=0)), axis=0)
 
-    def build(k, acc):
-        o, h, slot = place(k)
-
-        @pl.when((k > 0) & valid(o))
+    def next_block(k, last):
+        later = jnp.minimum(k + 1, last)
+        o, h, slot = place(later)
+
+        @pl.when((k < last) & valid(o))
         def _():
             wait_block(c0, 0, o, h)
 
+        return slot
+
+    def build(k, carry):
+        slot = place(k)[2]
+        upcoming = next_block(k, NEAR_SLOTS - 1)
         start = pl.multiple_of(k * OWN, OWN)
-        for t in range(CH):
-            column_coords(slot, t)
-        for t in range(CH):
-            for n in range(OWN // LANE):
-                lanes = slice(n * LANE, (n + 1) * LANE)
-                rx, ry, rz = rows[0:1, lanes], rows[1:2, lanes], rows[2:3, lanes]
-                for sub in range(LANE // SUB):
-                    hi, lo = split(tile(t, sub, rx, ry, rz))
-                    at = pl.ds(start + t * LANE + sub * SUB, SUB)
-                    kh[at, lanes] = hi
-                    kl[at, lanes] = lo
+
+        def multiply(t):
             v = near_values(slot, t)
             at = pl.ds(start + t * LANE, LANE)
-            acc = acc + jnp.dot(v, kh[at, :], preferred_element_type=f32)
-            acc = acc + jnp.dot(v, kl[at, :], preferred_element_type=f32)
-        return acc
-
-    acc = lax.fori_loop(0, NEAR_SLOTS, build, jnp.zeros((16, OWN), f32))
+            acc_near[...] += jnp.dot(v, kh[at, :], preferred_element_type=f32) + jnp.dot(
+                v, kl[at, :], preferred_element_type=f32
+            )
+
+        for t in range(CH):
+            fill(k, t, rsrc[...], kh, kl, start)
+            if t == 0:
+                column_terms(upcoming, k + 1)
+            if t > 0:
+                multiply(t - 1)
+        multiply(CH - 1)
+        return carry
+
+    column_terms(own, 0)
+    acc_near[...] = jnp.zeros_like(acc_near)
+    lax.fori_loop(0, NEAR_SLOTS, build, 0)
+    acc = acc_near[...]
     image = acc[0:8] + acc[8:16]
     first = image[0:3] - SHIFT * fmat[0:3, :]
     fmat[3:6, :] = first
@@ -351,6 +408,66 @@
 
     keep_own(f1, first)
     send_all(f1, 1)
+
+    def far_values(slot, t):
+        cc = c0[slot, 3 * t : 3 * t + 3, :]
+        parts = [
+            c0[slot, 16 + 3 * t : 16 + 3 * t + 3, :],
+            f1[slot, 3 * t : 3 * t + 3, :],
+            f2[slot, 3 * t : 3 * t + 3, :],
+            jnp.zeros((3, LANE), f32),
+        ]
+        parts += basis_rows(cc[0:1], cc[1:2], cc[2:3])
+        return jnp.concatenate(split(jnp.concatenate(parts, axis=0)), axis=0)
+
+    def target_fill(k, region, after):
+        o = place(k)[0]
+        start = pl.multiple_of(region * OWN, OWN)
+        for t in range(CH):
+            fill(k, t, rtgt[FAR + o], th, tl, start)
+            after(t, start)
+
+    def target_keep(k, carry):
+        target_fill(k, k, lambda t, start: None)
+        return carry
+
+    def target_multiply(slot, t, start):
+        v = far_values(slot, t)
+        at = pl.ds(start + t * LANE, LANE)
+        acc_far[...] += jnp.dot(v, th[at, :], preferred_element_type=f32) + jnp.dot(
+            v, tl[at, :], preferred_element_type=f32
+        )
+
+    def target_now(k, carry):
+        o, h, slot = place(k)
+
+        @pl.when((k >= NEAR_SLOTS) & valid(o))
+        def _():
+            wait_block(c0, 0, o, h)
+            wait_block(f1, 1, o, h)
+            wait_block(f2, 2, o, h)
+
+        @pl.when(k >= NEAR_SLOTS)
+        def _():
+            column_terms(slot, k)
+
+        def after(t, start):
+            if t > 0:
+                target_multiply(slot, t - 1, start)
+
+        target_fill(k, KEEP, after)
+        target_multiply(slot, CH - 1, pl.multiple_of(KEEP * OWN, OWN))
+        return carry
+
+    def target_kept(k, carry):
+        slot = place(k)[2]
+        start = pl.multiple_of(k * OWN, OWN)
+        v = jnp.concatenate([far_values(slot, t) for t in range(CH)], axis=1)
+        at = pl.ds(start, OWN)
+        acc_far[...] += jnp.dot(v, th[at, :], preferred_element_type=f32) + jnp.dot(
+            v, tl[at, :], preferred_element_type=f32
+        )
+        return carry
 
     def padded_split(v):
         v = jnp.concatenate([v, jnp.zeros((5, LANE), f32)], axis=0)
@@ -375,21 +492,24 @@
         acc = lax.fori_loop(0, NEAR_SLOTS, step, jnp.zeros((16, OWN), f32))
         return acc[0:3] + acc[8:11]
 
+    lax.fori_loop(0, KEEP // 2, target_keep, 0)
     second = apply_near(f1, 1) - SHIFT * first
     fmat[6:9, :] = second
     keep_own(f2, second)
     send_all(f2, 2)
+    lax.fori_loop(KEEP // 2, KEEP, target_keep, 0)
     third = apply_near(f2, 2) - SHIFT * second
     fmat[9:12, :] = third
 
     everything = fmat[...]
-    ga[zi] = lax.dot_general(
+    local = lax.dot_general(
         fmat[0:24, :],
         everything,
         (((1,), (1,)), ((), ())),
         precision=HIGH,
         preferred_element_type=f32,
     )
+    ga[zi] = local[0:8] + pltpu.roll(local[8:16], 32, 1) + pltpu.roll(local[16:24], 64, 1)
 
     def a_copy(d):
         q, h = ring_a[d - 1]
@@ -440,46 +560,9 @@
     for d in range(1, RING):
         a_copy(d).start()
 
-    def far_values(slot, t):
-        cc = c0[slot, 3 * t : 3 * t + 3, :]
-        parts = [
-            c0[slot, 16 + 3 * t : 16 + 3 * t + 3, :],
-            f1[slot, 3 * t : 3 * t + 3, :],
-            f2[slot, 3 * t : 3 * t + 3, :],
-            jnp.zeros((3, LANE), f32),
-        ]
-        parts += basis_rows(cc[0:1], cc[1:2], cc[2:3])
-        return jnp.concatenate(split(jnp.concatenate(parts, axis=0)), axis=0)
-
-    def target(k, acc):
-        o, h, slot = place(k)
-
-        @pl.when((k >= NEAR_SLOTS) & valid(o))
-        def _():
-            wait_block(c0, 0, o, h)
-            wait_block(f1, 1, o, h)
-            wait_block(f2, 2, o, h)
-
-        for t in range(CH):
-            column_coords(slot, t)
-        for t in range(CH):
-            for n in range(TGT // LANE):
-                lanes = slice(n * LANE, (n + 1) * LANE)
-                rx = trows[FAR + o, :, lanes]
-                ry, rz = trows[7, :, lanes], trows[8, :, lanes]
-                for sub in range(LANE // SUB):
-                    hi, lo = split(tile(t, sub, rx, ry, rz))
-                    at = slice(t * LANE + sub * SUB, t * LANE + (sub + 1) * SUB)
-                    th[at, lanes] = hi
-                    tl[at, lanes] = lo
-            v = far_values(slot, t)
-            at = slice(t * LANE, (t + 1) * LANE)
-            acc = acc + jnp.dot(v, th[at, :], preferred_element_type=f32)
-            acc = acc + jnp.dot(v, tl[at, :], preferred_element_type=f32)
-        return acc
-
-    half = FAR_SLOTS // 2
-    acc = lax.fori_loop(0, half, target, jnp.zeros((32, TGT), f32))
+    acc_far[...] = jnp.zeros_like(acc_far)
+    half = KEEP + (FAR_SLOTS - KEEP) // 2
+    lax.fori_loop(KEEP, half, target_now, 0)
 
     for d in range(1, RING):
         a_wait(d)
@@ -490,15 +573,19 @@
     for i in range(RING - 1):
         b_copy(i).start()
 
-    acc = lax.fori_loop(half, FAR_SLOTS, target, acc)
-    mmat[0:16, :] = acc[0:16] + acc[16:32]
+    lax.fori_loop(half, FAR_SLOTS, target_now, 0)
+    lax.fori_loop(0, KEEP, target_kept, 0)
+    mmat[0:16, :] = acc_far[0:16, :] + acc_far[16:32, :]
 
     for i in range(RING - 1):
         b_wait(i)
     whole = gb[0]
     for i in range(1, RING):
         whole = whole + gb[i]
-    gram = jnp.concatenate([whole, jnp.zeros((LANE - 24, LANE), f32)], axis=0)
+    few = lax.broadcasted_iota(jnp.int32, (8, LANE), 1) < 24
+    parts = [whole, pltpu.roll(whole, LANE - 32, 1), pltpu.roll(whole, LANE - 64, 1)]
+    parts = [jnp.where(few, part, 0.0) for part in parts]
+    gram = jnp.concatenate(parts + [jnp.zeros((LANE - 24, LANE), f32)], axis=0)
     head, tail = coefficients(gram)
     weights = jnp.dot(head, everything, precision=HIGH, preferred_element_type=f32)
     weights_ref[...] = weights[0:3]
@@ -534,15 +621,18 @@
             pltpu.VMEM((FAR_SLOTS, 16, LANE), f32),
             pltpu.VMEM((NEAR_SLOTS * OWN, OWN), bf16),
             pltpu.VMEM((NEAR_SLOTS * OWN, OWN), bf16),
-            pltpu.VMEM((OWN, TGT), bf16),
-            pltpu.VMEM((OWN, TGT), bf16),
-            pltpu.VMEM((CH, 3, LANE, LANE), f32),
-            pltpu.VMEM((8, OWN), f32),
-            pltpu.VMEM((9, 1, TGT), f32),
+            pltpu.VMEM(((KEEP + 1) * OWN, TGT), bf16),
+            pltpu.VMEM(((KEEP + 1) * OWN, TGT), bf16),
+            pltpu.VMEM((16, OWN), f32),
+            pltpu.VMEM((32, TGT), f32),
+            pltpu.VMEM((FAR_SLOTS * OWN, TERMS), bf16),
+            pltpu.VMEM((CH * TERMS, LANE), f32),
+            pltpu.VMEM((TERMS, OWN), bf16),
+            pltpu.VMEM((2 * FAR + 1, TERMS, TGT), bf16),
             pltpu.VMEM((LANE, OWN), f32),
             pltpu.VMEM((LANE, TGT), f32),
-            pltpu.VMEM((RING, 24, LANE), f32),
-            pltpu.VMEM((RING, 24, LANE), f32),
+            pltpu.VMEM((RING, 8, LANE), f32),
+            pltpu.VMEM((RING, 8, LANE), f32),
             dma((3, FAR_SLOTS)),
             dma((3, FAR_SLOTS)),
             dma((RING,)),

time: 97.8 us -> 91.3 us (0.934)
  Pallas kernels: 93.6 us -> 88 us
    pallas_call x1, Pallas kernels: 93.6 us -> 88 us  [shards(): pl.pallas_call(kernel, out_shape=(jax.ShapeDtypeStruct((3, OWN), f32), ja...]
where the time goes in v2:
time: 91.3 us; the launch traced here: 91.1 us
  Pallas kernels  88 us (96%)
  local copies, waits for them, and re-layouts  2.49 us (3%)
    pallas_call x1, Pallas kernels, shards(): pl.pallas_call(kernel, out_shape=(jax.ShapeDtypeStruct((3, OWN), f32), ja...  88 us
    unnamed x7, local copies, waits for them, and re-layouts  2.49 us

profile of v2, /device:TPU:1, one launch (start us, length us, event | category | flops | bytes accessed | tf_op | source)
XLA Modules:
  0.0 91.1 jit_solution(9642453923181580691)
XLA Ops:
  0.6 88.0 %shard_map.67 = (f32[3,640]{1,0:T(4,128)}, f32[3,4]{1,0:T(4,128)}, f32[3,512]{1,0:T(4,128)}) custom-call(f32[3,640]{1,0:T(4,128)} %coords_ref.1, f32[3,640]{1,0:T(4,128)} %values_ref.1, f32[3,512]{1,0:T(4,128)} %tcoords_ref.1, s32[1,512]{1,0:T(1,128)} %bitcast.1), custom_call_target="tpu_custom_call" | custom-call | tf_op jit(solution)/shard_map/pallas_call | solution.py:609
  88.6 0.0 copy-start.1
  88.6 0.0 copy-start
  88.6 1.3 %copy.10 = f32[3,640]{1,0:T(4,128)} copy(f32[3,640]{1,0:T(4,128)} %get-tuple-element.6) | data formatting | bytes 15360
  90.0 0.0 copy-done.1
  90.0 0.6 copy.11
  90.5 0.0 copy-done
  90.5 0.6 copy.12
Async XLA Ops:
  88.6 1.3 %copy-start.1 = (f32[3,4]{1,0:T(4,128)S(1)}, f32[3,4]{1,0:T(4,128)}, u32[]{:S(2)}) copy-start(f32[3,4]{1,0:T(4,128)} %get-tuple-element.7) | copy-start | bytes 148
  88.6 1.9 %copy-start = (f32[3,512]{1,0:T(4,128)S(1)}, f32[3,512]{1,0:T(4,128)}, u32[]{:S(2)}) copy-start(f32[3,512]{1,0:T(4,128)} %get-tuple-element.8) | copy-start | bytes 18436

commit v3 on v2

--- a/solution.py
+++ b/solution.py
@@ -31,8 +31,7 @@
 ROOT = 1.0 / math.sqrt(NSRC)
 NEAR_SLOTS = (2 * REACH + 1) * NG
 FAR_SLOTS = (2 * FAR + 1) * NG
-MAGIC = 49152.0
-KEEP = 14
+KEEP = 16
 f32 = jnp.float32
 bf16 = jnp.bfloat16
 HIGH = lax.Precision.HIGHEST
@@ -159,7 +158,9 @@
         for i in range(k + 1):
             head = head - column[i] * heads[i]
             tail = tail - column[i] * tails[i]
-        rest_gram = times_gram(head)
+        rest_gram = head_gram
+        for i in range(k + 1):
+            rest_gram = rest_gram - column[i] * grams[i]
         length = jnp.sqrt(total(rest_gram * head) + total(tail * tail) + TINY)
         column.append(length)
         hessenberg.append(column)
@@ -351,9 +352,7 @@
         at = pl.ds(pl.multiple_of(k * OWN, OWN) + t * LANE, LANE)
         put = pl.ds(start + t * LANE, LANE)
         e = jnp.exp2(jnp.dot(lt[at, :], right, preferred_element_type=f32))
-        hi = (e + MAGIC) - MAGIC
-        hi_ref[put, :] = hi.astype(bf16)
-        lo_ref[put, :] = (e - hi).astype(bf16)
+        hi_ref[put, :], lo_ref[put, :] = split(e)
 
     def near_values(slot, t):
         cc = c0[slot, 3 * t : 3 * t + 3, :]
@@ -373,29 +372,37 @@
         return slot
 
     def build(k, carry):
-        slot = place(k)[2]
         upcoming = next_block(k, NEAR_SLOTS - 1)
         start = pl.multiple_of(k * OWN, OWN)
-
-        def multiply(t):
-            v = near_values(slot, t)
-            at = pl.ds(start + t * LANE, LANE)
-            acc_near[...] += jnp.dot(v, kh[at, :], preferred_element_type=f32) + jnp.dot(
-                v, kl[at, :], preferred_element_type=f32
-            )
 
         for t in range(CH):
             fill(k, t, rsrc[...], kh, kl, start)
             if t == 0:
                 column_terms(upcoming, k + 1)
-            if t > 0:
-                multiply(t - 1)
-        multiply(CH - 1)
         return carry
 
     column_terms(own, 0)
+    lax.fori_loop(0, NEAR_SLOTS, build, 0)
+
+    def blocks(m):
+        return place(m * NG)[0], [place(m * NG + i)[2] for i in range(NG)]
+
+    def product(hi_ref, lo_ref, region, values):
+        v = jnp.concatenate(values, axis=1)
+        at = pl.ds(pl.multiple_of(region * SLAB, SLAB), SLAB)
+        return jnp.dot(v, hi_ref[at, :], preferred_element_type=f32) + jnp.dot(
+            v, lo_ref[at, :], preferred_element_type=f32
+        )
+
+    def apply_first(m, carry):
+        slots = blocks(m)[1]
+        acc_near[...] += product(
+            kh, kl, m, [near_values(slot, t) for slot in slots for t in range(CH)]
+        )
+        return carry
+
     acc_near[...] = jnp.zeros_like(acc_near)
-    lax.fori_loop(0, NEAR_SLOTS, build, 0)
+    lax.fori_loop(0, 2 * REACH + 1, apply_first, 0)
     acc = acc_near[...]
     image = acc[0:8] + acc[8:16]
     first = image[0:3] - SHIFT * fmat[0:3, :]
@@ -420,53 +427,37 @@
         parts += basis_rows(cc[0:1], cc[1:2], cc[2:3])
         return jnp.concatenate(split(jnp.concatenate(parts, axis=0)), axis=0)
 
-    def target_fill(k, region, after):
-        o = place(k)[0]
-        start = pl.multiple_of(region * OWN, OWN)
-        for t in range(CH):
-            fill(k, t, rtgt[FAR + o], th, tl, start)
-            after(t, start)
-
-    def target_keep(k, carry):
-        target_fill(k, k, lambda t, start: None)
-        return carry
-
-    def target_multiply(slot, t, start):
-        v = far_values(slot, t)
-        at = pl.ds(start + t * LANE, LANE)
-        acc_far[...] += jnp.dot(v, th[at, :], preferred_element_type=f32) + jnp.dot(
-            v, tl[at, :], preferred_element_type=f32
-        )
-
-    def target_now(k, carry):
+    def target_build(first):
+        def step(k, carry):
+            o = place(k)[0]
+            start = pl.multiple_of((k - first) * OWN, OWN)
+            for t in range(CH):
+                fill(k, t, rtgt[FAR + o], th, tl, start)
+            return carry
+
+        return step
+
+    def target_apply(first):
+        def step(m, carry):
+            slots = blocks(m)[1]
+            acc_far[...] += product(
+                th,
+                tl,
+                m - first,
+                [far_values(slot, t) for slot in slots for t in range(CH)],
+            )
+            return carry
+
+        return step
+
+    def last_terms(k, carry):
         o, h, slot = place(k)
 
-        @pl.when((k >= NEAR_SLOTS) & valid(o))
+        @pl.when(valid(o))
         def _():
             wait_block(c0, 0, o, h)
-            wait_block(f1, 1, o, h)
-            wait_block(f2, 2, o, h)
-
-        @pl.when(k >= NEAR_SLOTS)
-        def _():
-            column_terms(slot, k)
-
-        def after(t, start):
-            if t > 0:
-                target_multiply(slot, t - 1, start)
-
-        target_fill(k, KEEP, after)
-        target_multiply(slot, CH - 1, pl.multiple_of(KEEP * OWN, OWN))
-        return carry
-
-    def target_kept(k, carry):
-        slot = place(k)[2]
-        start = pl.multiple_of(k * OWN, OWN)
-        v = jnp.concatenate([far_values(slot, t) for t in range(CH)], axis=1)
-        at = pl.ds(start, OWN)
-        acc_far[...] += jnp.dot(v, th[at, :], preferred_element_type=f32) + jnp.dot(
-            v, tl[at, :], preferred_element_type=f32
-        )
+
+        column_terms(slot, k)
         return carry
 
     def padded_split(v):
@@ -474,30 +465,38 @@
         return jnp.concatenate(split(v), axis=0)
 
     def apply_near(buf, which):
-        def step(k, acc):
-            o, h, slot = place(k)
-
-            @pl.when((k > 0) & valid(o))
-            def _():
-                wait_block(buf, which, o, h)
-
-            start = pl.multiple_of(k * OWN, OWN)
-            v = jnp.concatenate(
-                [padded_split(buf[slot, 3 * t : 3 * t + 3, :]) for t in range(CH)], axis=1
+        def step(m, carry):
+            o, slots = blocks(m)
+            for i in range(NG):
+                h = place(m * NG + i)[1]
+
+                @pl.when((m * NG + i > 0) & valid(o))
+                def _():
+                    wait_block(buf, which, o, h)
+
+            acc_near[...] += product(
+                kh,
+                kl,
+                m,
+                [
+                    padded_split(buf[slot, 3 * t : 3 * t + 3, :])
+                    for slot in slots
+                    for t in range(CH)
+                ],
             )
-            at = pl.ds(start, OWN)
-            acc = acc + jnp.dot(v, kh[at, :], preferred_element_type=f32)
-            return acc + jnp.dot(v, kl[at, :], preferred_element_type=f32)
-
-        acc = lax.fori_loop(0, NEAR_SLOTS, step, jnp.zeros((16, OWN), f32))
-        return acc[0:3] + acc[8:11]
-
-    lax.fori_loop(0, KEEP // 2, target_keep, 0)
+            return carry
+
+        acc_near[...] = jnp.zeros_like(acc_near)
+        lax.fori_loop(0, 2 * REACH + 1, step, 0)
+        return acc_near[0:3, :] + acc_near[8:11, :]
+
+    lax.fori_loop(NEAR_SLOTS, FAR_SLOTS, last_terms, 0)
+    lax.fori_loop(0, KEEP // 2, target_build(0), 0)
     second = apply_near(f1, 1) - SHIFT * first
     fmat[6:9, :] = second
     keep_own(f2, second)
     send_all(f2, 2)
-    lax.fori_loop(KEEP // 2, KEEP, target_keep, 0)
+    lax.fori_loop(KEEP // 2, KEEP, target_build(0), 0)
     third = apply_near(f2, 2) - SHIFT * second
     fmat[9:12, :] = third
 
@@ -561,8 +560,10 @@
         a_copy(d).start()
 
     acc_far[...] = jnp.zeros_like(acc_far)
-    half = KEEP + (FAR_SLOTS - KEEP) // 2
-    lax.fori_loop(KEEP, half, target_now, 0)
+    kept = KEEP // NG
+    middle = KEEP + 2 * (FAR_SLOTS - KEEP) // 3
+    lax.fori_loop(0, kept, target_apply(0), 0)
+    lax.fori_loop(KEEP, middle, target_build(KEEP), 0)
 
     for d in range(1, RING):
         a_wait(d)
@@ -573,8 +574,16 @@
     for i in range(RING - 1):
         b_copy(i).start()
 
-    lax.fori_loop(half, FAR_SLOTS, target_now, 0)
-    lax.fori_loop(0, KEEP, target_kept, 0)
+    lax.fori_loop(middle, FAR_SLOTS, target_build(KEEP), 0)
+    for o in (FAR, -FAR):
+        for h in range(NG):
+
+            @pl.when(valid(o))
+            def _():
+                wait_block(f1, 1, o, h)
+                wait_block(f2, 2, o, h)
+
+    lax.fori_loop(kept, 2 * FAR + 1, target_apply(kept), 0)
     mmat[0:16, :] = acc_far[0:16, :] + acc_far[16:32, :]
 
     for i in range(RING - 1):
@@ -621,8 +630,8 @@
             pltpu.VMEM((FAR_SLOTS, 16, LANE), f32),
             pltpu.VMEM((NEAR_SLOTS * OWN, OWN), bf16),
             pltpu.VMEM((NEAR_SLOTS * OWN, OWN), bf16),
-            pltpu.VMEM(((KEEP + 1) * OWN, TGT), bf16),
-            pltpu.VMEM(((KEEP + 1) * OWN, TGT), bf16),
+            pltpu.VMEM((KEEP * OWN, TGT), bf16),
+            pltpu.VMEM((KEEP * OWN, TGT), bf16),
             pltpu.VMEM((16, OWN), f32),
             pltpu.VMEM((32, TGT), f32),
             pltpu.VMEM((FAR_SLOTS * OWN, TERMS), bf16),

time: 91.3 us -> 72.9 us (0.80)
  Pallas kernels: 88 us -> 69.5 us
    pallas_call x1, Pallas kernels: 88 us -> 69.5 us  [shards(): pl.pallas_call(kernel, out_shape=(jax.ShapeDtypeStruct((3, OWN), f32), ja...]
where the time goes in v3:
time: 72.9 us; the launch traced here: 72.7 us
  Pallas kernels  69.5 us (95%)
  local copies, waits for them, and re-layouts  2.49 us (3%)
    pallas_call x1, Pallas kernels, shards(): pl.pallas_call(kernel, out_shape=(jax.ShapeDtypeStruct((3, OWN), f32), ja...  69.5 us
    unnamed x7, local copies, waits for them, and re-layouts  2.49 us

profile of v3, /device:TPU:1, one launch (start us, length us, event | category | flops | bytes accessed | tf_op | source)
XLA Modules:
  0.0 72.7 jit_solution(13623216109820783791)
XLA Ops:
  0.6 69.5 %shard_map.67 = (f32[3,640]{1,0:T(4,128)}, f32[3,4]{1,0:T(4,128)}, f32[3,512]{1,0:T(4,128)}) custom-call(f32[3,640]{1,0:T(4,128)} %coords_ref.1, f32[3,640]{1,0:T(4,128)} %values_ref.1, f32[3,512]{1,0:T(4,128)} %tcoords_ref.1, s32[1,512]{1,0:T(1,128)} %bitcast.1), custom_call_target="tpu_custom_call" | custom-call | tf_op jit(solution)/shard_map/pallas_call | solution.py:618
  70.2 0.0 copy-start.1
  70.2 0.0 copy-start
  70.2 1.3 %copy.10 = f32[3,640]{1,0:T(4,128)} copy(f32[3,640]{1,0:T(4,128)} %get-tuple-element.6) | data formatting | bytes 15360
  71.5 0.0 copy-done.1
  71.5 0.6 copy.11
  72.1 0.0 copy-done
  72.1 0.6 copy.12
Async XLA Ops:
  70.2 1.3 %copy-start.1 = (f32[3,4]{1,0:T(4,128)S(1)}, f32[3,4]{1,0:T(4,128)}, u32[]{:S(2)}) copy-start(f32[3,4]{1,0:T(4,128)} %get-tuple-element.7) | copy-start | bytes 148
  70.2 1.9 %copy-start = (f32[3,512]{1,0:T(4,128)S(1)}, f32[3,512]{1,0:T(4,128)}, u32[]{:S(2)}) copy-start(f32[3,512]{1,0:T(4,128)} %get-tuple-element.8) | copy-start | bytes 18436

commit v4 on v3

--- a/solution.py
+++ b/solution.py
@@ -181,9 +181,7 @@
     values_ref,
     tcoords_ref,
     owner_ref,
-    weights_ref,
-    poly_ref,
-    mapped_ref,
+    out_ref,
     c0,
     f1,
     f2,
@@ -193,8 +191,10 @@
     tl,
     acc_near,
     acc_far,
-    lt,
-    stage,
+    lt_even,
+    lt_odd,
+    stage_even,
+    stage_odd,
     rsrc,
     rtgt,
     fmat,
@@ -253,12 +253,79 @@
         lanes = slice(t * LANE, (t + 1) * LANE)
         c0[own, 3 * t : 3 * t + 3, :] = coords_ref[:, lanes]
         c0[own, 16 + 3 * t : 16 + 3 * t + 3, :] = values_ref[:, lanes]
+    absent = jnp.where(
+        lax.broadcasted_iota(jnp.int32, (32, LANE), 0) % 3 == 0, 1e5, 0.0
+    )
+    absent = jnp.where(lax.broadcasted_iota(jnp.int32, (32, LANE), 0) < 15, absent, 0.0)
+    for o in range(-FAR, FAR + 1):
+        if o != 0:
+
+            @pl.when(jnp.logical_not(valid(o)))
+            def _():
+                for h in range(NG):
+                    slot = (FAR + o) * NG + h
+                    c0[slot] = absent
+                    f1[slot] = jnp.zeros((16, LANE), f32)
+                    f2[slot] = jnp.zeros((16, LANE), f32)
+
+    pl.semaphore_wait(barrier, expected)
+
+    def block_copy(buf, which, o, h):
+        return pltpu.make_async_remote_copy(
+            src_ref=buf.at[own],
+            dst_ref=buf.at[(FAR - o) * NG + g],
+            send_sem=send_sem.at[which, (FAR + o) * NG + h],
+            recv_sem=recv_sem.at[which, (FAR - o) * NG + g],
+            device_id=(p + o, h),
+            device_id_type=MESH,
+        )
+
+    def send_all(buf, which, far):
+        for o, h in halo:
+            if (abs(o) == FAR) != far:
+                continue
+            copy = block_copy(buf, which, o, h)
+            if o == 0:
+                copy.start()
+            else:
+                pl.when(valid(o))(copy.start)
+
+    def wait_send_all(buf, which):
+        for o, h in halo:
+            copy = block_copy(buf, which, o, h)
+            if o == 0:
+                copy.wait_send()
+            else:
+                pl.when(valid(o))(copy.wait_send)
+
+    def wait_block(buf, which, o, h):
+        slot = (FAR + o) * NG + h
+        pltpu.make_async_remote_copy(
+            src_ref=buf.at[own],
+            dst_ref=buf.at[slot],
+            send_sem=send_sem.at[which, slot],
+            recv_sem=recv_sem.at[which, slot],
+            device_id=(p + o, h),
+            device_id_type=MESH,
+        ).wait_recv()
+
+    def place(k):
+        oi = lax.div(k, NG)
+        dist = lax.div(oi + 1, 2)
+        o = jnp.where(lax.rem(oi, 2) == 1, dist, -dist)
+        h = lax.rem(g + k, NG)
+        return o, h, (FAR + o) * NG + h
+
+    send_all(c0, 0, False)
+
     base = p.astype(f32)
     sx, sy, sz = coords_ref[0:1, :], coords_ref[1:2, :], coords_ref[2:3, :]
     source_terms = point_terms((sx - base) * XSCALE, sy, sz, False, jnp.zeros_like(sx))
     source_terms += [jnp.zeros_like(sx)] * (TERMS - len(source_terms))
     rsrc[...] = jnp.concatenate(source_terms, axis=0).astype(bf16)
-    stage[...] = jnp.zeros_like(stage)
+    for stage in (stage_even, stage_odd):
+        stage[...] = jnp.zeros_like(stage)
+    sides = ((lt_even, stage_even), (lt_odd, stage_odd))
     fmat[...] = jnp.zeros_like(fmat)
     mmat[...] = jnp.zeros_like(mmat)
     fmat[0:3, :] = values_ref[...]
@@ -277,82 +344,22 @@
     for i, part in enumerate(basis_rows(tx, ty, tz)):
         mmat[24 + i : 25 + i, :] = part
 
-    absent = jnp.where(
-        lax.broadcasted_iota(jnp.int32, (32, LANE), 0) % 3 == 0, 1e5, 0.0
-    )
-    absent = jnp.where(lax.broadcasted_iota(jnp.int32, (32, LANE), 0) < 15, absent, 0.0)
-    for o in range(-FAR, FAR + 1):
-        if o != 0:
-
-            @pl.when(jnp.logical_not(valid(o)))
-            def _():
-                for h in range(NG):
-                    slot = (FAR + o) * NG + h
-                    c0[slot] = absent
-                    f1[slot] = jnp.zeros((16, LANE), f32)
-                    f2[slot] = jnp.zeros((16, LANE), f32)
-
-    pl.semaphore_wait(barrier, expected)
-
-    def block_copy(buf, which, o, h):
-        return pltpu.make_async_remote_copy(
-            src_ref=buf.at[own],
-            dst_ref=buf.at[(FAR - o) * NG + g],
-            send_sem=send_sem.at[which, (FAR + o) * NG + h],
-            recv_sem=recv_sem.at[which, (FAR - o) * NG + g],
-            device_id=(p + o, h),
-            device_id_type=MESH,
-        )
-
-    def send_all(buf, which):
-        for o, h in halo:
-            copy = block_copy(buf, which, o, h)
-            if o == 0:
-                copy.start()
-            else:
-                pl.when(valid(o))(copy.start)
-
-    def wait_send_all(buf, which):
-        for o, h in halo:
-            copy = block_copy(buf, which, o, h)
-            if o == 0:
-                copy.wait_send()
-            else:
-                pl.when(valid(o))(copy.wait_send)
-
-    def wait_block(buf, which, o, h):
-        slot = (FAR + o) * NG + h
-        pltpu.make_async_remote_copy(
-            src_ref=buf.at[own],
-            dst_ref=buf.at[slot],
-            send_sem=send_sem.at[which, slot],
-            recv_sem=recv_sem.at[which, slot],
-            device_id=(p + o, h),
-            device_id_type=MESH,
-        ).wait_recv()
-
-    def place(k):
-        oi = lax.div(k, NG)
-        dist = lax.div(oi + 1, 2)
-        o = jnp.where(lax.rem(oi, 2) == 1, dist, -dist)
-        h = lax.rem(g + k, NG)
-        return o, h, (FAR + o) * NG + h
-
-    send_all(c0, 0)
-
-    def column_terms(slot, k):
+
+    def column_terms(slot, pair, side):
+        lt, stage = sides[side]
         x, y, z = (c0[slot, pl.ds(i, CH, stride=3), :] for i in range(3))
         for i, v in enumerate(point_terms((x - base) * XSCALE, y, z, True, None)):
             stage[pl.ds(i, CH, stride=TERMS), :] = v
         for t in range(CH):
-            at = pl.ds(pl.multiple_of(k * OWN, OWN) + t * LANE, LANE)
+            at = pl.ds(pl.multiple_of(pair * OWN, OWN) + t * LANE, LANE)
             lt[at, :] = stage[t * TERMS : (t + 1) * TERMS, :].T.astype(bf16)
 
-    def fill(k, t, right, hi_ref, lo_ref, start):
-        at = pl.ds(pl.multiple_of(k * OWN, OWN) + t * LANE, LANE)
-        put = pl.ds(start + t * LANE, LANE)
-        e = jnp.exp2(jnp.dot(lt[at, :], right, preferred_element_type=f32))
-        hi_ref[put, :], lo_ref[put, :] = split(e)
+    def fill(pair, side, right, hi_ref, lo_ref, start):
+        for t in range(CH):
+            at = pl.ds(pl.multiple_of(pair * OWN, OWN) + t * LANE, LANE)
+            put = pl.ds(start + t * LANE, LANE)
+            e = jnp.exp2(jnp.dot(sides[side][0][at, :], right, preferred_element_type=f32))
+            hi_ref[put, :], lo_ref[put, :] = split(e)
 
     def near_values(slot, t):
         cc = c0[slot, 3 * t : 3 * t + 3, :]
@@ -361,28 +368,27 @@
         parts.append(jnp.zeros((1, LANE), f32))
         return jnp.concatenate(split(jnp.concatenate(parts, axis=0)), axis=0)
 
-    def next_block(k, last):
-        later = jnp.minimum(k + 1, last)
-        o, h, slot = place(later)
-
-        @pl.when((k < last) & valid(o))
+    def arrived(k, last):
+        o, h, slot = place(jnp.minimum(k, last))
+
+        @pl.when((k <= last) & valid(o))
         def _():
             wait_block(c0, 0, o, h)
 
         return slot
 
-    def build(k, carry):
-        upcoming = next_block(k, NEAR_SLOTS - 1)
-        start = pl.multiple_of(k * OWN, OWN)
-
-        for t in range(CH):
-            fill(k, t, rsrc[...], kh, kl, start)
-            if t == 0:
-                column_terms(upcoming, k + 1)
+    def build(pair, carry):
+        odd = arrived(2 * pair + 1, NEAR_SLOTS - 1)
+        even = arrived(2 * pair + 2, NEAR_SLOTS - 1)
+        start = pl.multiple_of(pair * 2 * OWN, 2 * OWN)
+        column_terms(odd, pair, 1)
+        fill(pair, 0, rsrc[...], kh, kl, start)
+        column_terms(even, pair + 1, 0)
+        fill(pair, 1, rsrc[...], kh, kl, start + OWN)
         return carry
 
-    column_terms(own, 0)
-    lax.fori_loop(0, NEAR_SLOTS, build, 0)
+    column_terms(own, 0, 0)
+    lax.fori_loop(0, NEAR_SLOTS // 2, build, 0)
 
     def blocks(m):
         return place(m * NG)[0], [place(m * NG + i)[2] for i in range(NG)]
@@ -414,7 +420,9 @@
             buf[own, 3 * t : 3 * t + 3, :] = v[:, t * LANE : (t + 1) * LANE]
 
     keep_own(f1, first)
-    send_all(f1, 1)
+    send_all(f1, 1, False)
+    send_all(c0, 0, True)
+    send_all(f1, 1, True)
 
     def far_values(slot, t):
         cc = c0[slot, 3 * t : 3 * t + 3, :]
@@ -428,11 +436,11 @@
         return jnp.concatenate(split(jnp.concatenate(parts, axis=0)), axis=0)
 
     def target_build(first):
-        def step(k, carry):
-            o = place(k)[0]
-            start = pl.multiple_of((k - first) * OWN, OWN)
-            for t in range(CH):
-                fill(k, t, rtgt[FAR + o], th, tl, start)
+        def step(pair, carry):
+            start = pl.multiple_of((2 * pair - first) * OWN, 2 * OWN)
+            right = rtgt[FAR + place(2 * pair)[0]]
+            fill(pair, 0, right, th, tl, start)
+            fill(pair, 1, right, th, tl, start + OWN)
             return carry
 
         return step
@@ -450,14 +458,11 @@
 
         return step
 
-    def last_terms(k, carry):
-        o, h, slot = place(k)
-
-        @pl.when(valid(o))
-        def _():
-            wait_block(c0, 0, o, h)
-
-        column_terms(slot, k)
+    def last_terms(pair, carry):
+        even = arrived(2 * pair, FAR_SLOTS - 1)
+        odd = arrived(2 * pair + 1, FAR_SLOTS - 1)
+        column_terms(even, pair, 0)
+        column_terms(odd, pair, 1)
         return carry
 
     def padded_split(v):
@@ -490,13 +495,14 @@
         lax.fori_loop(0, 2 * REACH + 1, step, 0)
         return acc_near[0:3, :] + acc_near[8:11, :]
 
-    lax.fori_loop(NEAR_SLOTS, FAR_SLOTS, last_terms, 0)
-    lax.fori_loop(0, KEEP // 2, target_build(0), 0)
+    lax.fori_loop(0, KEEP // 4, target_build(0), 0)
     second = apply_near(f1, 1) - SHIFT * first
     fmat[6:9, :] = second
     keep_own(f2, second)
-    send_all(f2, 2)
-    lax.fori_loop(KEEP // 2, KEEP, target_build(0), 0)
+    send_all(f2, 2, False)
+    send_all(f2, 2, True)
+    lax.fori_loop(KEEP // 4, KEEP // 2, target_build(0), 0)
+    lax.fori_loop(NEAR_SLOTS // 2, FAR_SLOTS // 2, last_terms, 0)
     third = apply_near(f2, 2) - SHIFT * second
     fmat[9:12, :] = third
 
@@ -563,7 +569,7 @@
     kept = KEEP // NG
     middle = KEEP + 2 * (FAR_SLOTS - KEEP) // 3
     lax.fori_loop(0, kept, target_apply(0), 0)
-    lax.fori_loop(KEEP, middle, target_build(KEEP), 0)
+    lax.fori_loop(KEEP // 2, middle // 2, target_build(KEEP), 0)
 
     for d in range(1, RING):
         a_wait(d)
@@ -574,7 +580,7 @@
     for i in range(RING - 1):
         b_copy(i).start()
 
-    lax.fori_loop(middle, FAR_SLOTS, target_build(KEEP), 0)
+    lax.fori_loop(middle // 2, FAR_SLOTS // 2, target_build(KEEP), 0)
     for o in (FAR, -FAR):
         for h in range(NG):
 
@@ -597,11 +603,11 @@
     gram = jnp.concatenate(parts + [jnp.zeros((LANE - 24, LANE), f32)], axis=0)
     head, tail = coefficients(gram)
     weights = jnp.dot(head, everything, precision=HIGH, preferred_element_type=f32)
-    weights_ref[...] = weights[0:3]
-    poly_ref[...] = pltpu.roll(tail, LANE - 12, 1)[0:3, 0:4]
+    out_ref[:, 0:OWN] = weights
+    out_ref[:, OWN + TGT :] = pltpu.roll(tail, LANE - 12, 1)
     both = head + pltpu.roll(tail, 12, 1)
     mapped = jnp.dot(both, mmat[...], precision=HIGH, preferred_element_type=f32)
-    mapped_ref[...] = mapped[0:3]
+    out_ref[:, OWN : OWN + TGT] = mapped
 
     wait_send_all(c0, 0)
     wait_send_all(f1, 1)
@@ -612,18 +618,20 @@
         b_copy(i).wait_send()
 
 
+def unpack(packed_ref, weights_ref, poly_ref, mapped_ref):
+    weights_ref[...] = packed_ref[0:3, 0:OWN]
+    mapped_ref[...] = packed_ref[0:3, OWN : OWN + TGT]
+    poly_ref[...] = packed_ref[0:3, OWN + TGT : OWN + TGT + 4]
+
+
 def shards(source_coords, source_values, target_coords, target_owner):
     vmem = pl.BlockSpec(memory_space=pltpu.VMEM)
     dma = pltpu.SemaphoreType.DMA
-    return pl.pallas_call(
+    packed = pl.pallas_call(
         kernel,
-        out_shape=(
-            jax.ShapeDtypeStruct((3, OWN), f32),
-            jax.ShapeDtypeStruct((3, 4), f32),
-            jax.ShapeDtypeStruct((3, TGT), f32),
-        ),
+        out_shape=jax.ShapeDtypeStruct((8, OWN + TGT + LANE), f32),
         in_specs=[vmem] * 4,
-        out_specs=(vmem,) * 3,
+        out_specs=vmem,
         scratch_shapes=[
             pltpu.VMEM((FAR_SLOTS, 32, LANE), f32),
             pltpu.VMEM((FAR_SLOTS, 16, LANE), f32),
@@ -634,7 +642,9 @@
             pltpu.VMEM((KEEP * OWN, TGT), bf16),
             pltpu.VMEM((16, OWN), f32),
             pltpu.VMEM((32, TGT), f32),
-            pltpu.VMEM((FAR_SLOTS * OWN, TERMS), bf16),
+            pltpu.VMEM((FAR_SLOTS // 2 * OWN, TERMS), bf16),
+            pltpu.VMEM((FAR_SLOTS // 2 * OWN, TERMS), bf16),
+            pltpu.VMEM((CH * TERMS, LANE), f32),
             pltpu.VMEM((CH * TERMS, LANE), f32),
             pltpu.VMEM((TERMS, OWN), bf16),
             pltpu.VMEM((2 * FAR + 1, TERMS, TGT), bf16),
@@ -653,6 +663,16 @@
             collective_id=0, has_side_effects=True, vmem_limit_bytes=62 * 1024 * 1024
         ),
     )(source_coords, source_values, target_coords, target_owner.reshape(1, TGT))
+    return pl.pallas_call(
+        unpack,
+        out_shape=(
+            jax.ShapeDtypeStruct((3, OWN), f32),
+            jax.ShapeDtypeStruct((3, 4), f32),
+            jax.ShapeDtypeStruct((3, TGT), f32),
+        ),
+        in_specs=[vmem],
+        out_specs=(vmem,) * 3,
+    )(packed)
 
 
 def solution(mesh):

time: 72.9 us -> 66 us (0.905)
  Pallas kernels: 69.5 us -> 65.1 us
  local copies, waits for them, and re-layouts: 2.49 us -> 0 us
    pallas_call x1 -> x2, Pallas kernels: 69.5 us -> 65.1 us  [the longest x1 63.8 us: shards(): pl.pallas_call(kernel, out_shape=jax.ShapeDtypeStruct((8, OWN + TGT + LAN...]
    unnamed x7 -> x0, local copies, waits for them, and re-layouts: 2.49 us -> none
where the time goes in v4:
time: 66 us; the launch traced here: 65.8 us
  Pallas kernels  65.1 us (99%)
    pallas_call x1, Pallas kernels, shards(): pl.pallas_call(kernel, out_shape=jax.ShapeDtypeStruct((8, OWN + TGT + LAN...  63.8 us
    pallas_call x1, Pallas kernels, shards(): pl.pallas_call(unpack, out_shape=(jax.ShapeDtypeStruct((3, OWN), f32), ja...  1.39 us

profile of v4, /device:TPU:1, one launch (start us, length us, event | category | flops | bytes accessed | tf_op | source)
XLA Modules:
  0.0 65.8 jit_solution(3384325154696216860)
XLA Ops:
  0.6 63.8 %shard_map.67.packed_ref = f32[8,1280]{1,0:T(8,128)} custom-call(f32[3,640]{1,0:T(4,128)} %coords_ref.1, f32[3,640]{1,0:T(4,128)} %values_ref.1, f32[3,512]{1,0:T(4,128)} %tcoords_ref.1, s32[1,512]{1,0:T(1,128)} %bitcast.1), custom_call_target="tpu_custom_call" | custom-call | tf_op jit(solution)/shard_map/pallas_call | solution.py:630
  64.4 1.4 %shard_map.68 = (f32[3,640]{1,0:T(4,128)}, f32[3,4]{1,0:T(4,128)}, f32[3,512]{1,0:T(4,128)}) custom-call(f32[8,1280]{1,0:T(8,128)} %shard_map.67.packed_ref), custom_call_target="tpu_custom_call" | custom-call | tf_op jit(solution)/shard_map/pallas_call | solution.py:666
